TPU v7x, 32 devices: a whole 2x2x4 slice. The times are simulated.
32 devices in a mesh: term: 16 (over z, x, core), sector: 2 (over y).
Axes of the slice: x: 2, y: 2, z: 4, core: 2. Of those that a mesh axis runs over, the one named last changes fastest.
Arguments:
- wavefunction: bfloat16 [4, 512, 512], P('sector'), may hold values from -6 to 6
- left_operators: bfloat16 [256, 512, 512], P(('term', 'sector')), may hold values from -0.25 to 0.25
- right_operators: bfloat16 [256, 512, 512], P(('term', 'sector')), may hold values from -0.25 to 0.25
- source_sector: int32 [256], P(('term', 'sector')), may hold values from 0 to 3
- target_sector: int32 [256], P(('term', 'sector')), may hold values from 0 to 3
- live_terms: int32 [32], P(('term', 'sector')), may hold values from 1 to 8, as said below
- sector_rows: int32 [4], replicated, may hold values from 1 to 512, as said below
Outputs:
- sigma_blocks: float32 [4, 512, 512], P('sector', 'term')
Inputs may be any that keep to these rules, and one draw needn't show every extreme that they name: Term group g = term index * 2 + sector index holds the term slots g * 8 to (g + 1) * 8 - 1; its live slots are the first live_terms[g]; some group has exactly 8. `sector_rows`: some sector uses exactly 512 rows.
All inputs are finite; a program needn't handle non-finite values.
Results may differ from a plain program's by a relative error of at most 0.0029.
Values may be sent and summed in bfloat16 or wider, within the bound.
A program may use at most 128 MiB of HBM per device.

v0:
```python
import functools

import jax
import jax.numpy as jnp
from jax import lax
from jax.experimental import pallas as pl
from jax.experimental.pallas import tpu as pltpu
from jax.sharding import PartitionSpec as P

BF16 = jnp.bfloat16
F32 = jnp.float32


def kernel(
    dims,
    wave,
    left,
    right,
    source_ref,
    target_ref,
    live_ref,
    rows_ref,
    out,
    near,
    far,
    lbuf,
    rbuf,
    prod,
    snd_a0,
    snd_b0,
    rcv_a0,
    rcv_b0,
    acc_a,
    acc_b,
    snd_a1,
    rcv_a1,
    snd_b1,
    rcv_b1,
    snd_a2,
    rcv_a2,
    snd_b2,
    rcv_b2,
    snd_a3,
    rcv_a3,
    snd_b3,
    rcv_b3,
    order,
    joins,
    load_sem,
    g_send,
    g_recv,
    h_send,
    h_recv,
    f_send,
    f_recv,
    s0,
    r0,
    sx,
    rx,
    sy_b,
    ry_b,
    sy_a,
    ry_a,
    sz,
    rz,
):
    Z, X, S, K, B, C = dims
    H, Q = C // 2, C // 4
    R = wave.shape[1]
    slots = left.shape[0]
    term = lax.axis_index("term")
    ym = lax.axis_index("sector")
    cm = lax.rem(term, 2)
    xm = lax.rem(term // 2, X)
    zm = term // (2 * X)
    co = 1 - cm
    xo = 1 - xm

    def dev(z, x, c, y):
        return ((z * X + x) * 2 + c, y)

    core_peer = dev(zm, xm, co, ym)
    x_peer = dev(zm, xo, cm, ym)

    def y_peer(d):
        return dev(zm, xm, cm, lax.rem(ym + d, S))

    def z_peer(d):
        return dev(lax.rem(zm + d, Z), xm, cm, ym)

    def remote(src, dst, ssem, rsem, peer):
        return pltpu.make_async_remote_copy(
            src_ref=src,
            dst_ref=dst,
            send_sem=ssem,
            recv_sem=rsem,
            device_id=peer,
            device_id_type=pl.DeviceIdType.MESH,
        )

    mine = pl.ds(ym * K, K)
    own_loads = []
    for n, (half, held) in enumerate(((xm, near), (xo, far))):
        cols = pl.ds(pl.multiple_of(half * H, 128), H)
        own_loads.append(
            pltpu.make_async_copy(wave.at[:, :, cols], held.at[mine], load_sem.at[n])
        )
    l_loads = [
        pltpu.make_async_copy(left.at[:, :, c], lbuf.at[:, c], load_sem.at[2 + c]) for c in range(2)
    ]
    l_loads += [
        pltpu.make_async_copy(right.at[:, :, h * H : (h + 1) * H], rbuf.at[h], load_sem.at[4 + h])
        for h in range(2)
    ]
    for cp in own_loads:
        cp.start()
    for cp in l_loads:
        cp.start()

    barrier = pltpu.get_barrier_semaphore()
    peers = [core_peer, x_peer]
    peers += [y_peer(d) for d in range(1, S)]
    peers += [z_peer(d) for d in range(1, Z)]
    for peer in peers:
        pl.semaphore_signal(barrier, inc=1, device_id=peer, device_id_type=pl.DeviceIdType.MESH)
    pl.semaphore_wait(barrier, len(peers))

    def part(held, d, j, c):
        sector = lax.rem(ym + S - d, S) * K + j // 4
        rows = pl.ds((j % 4) * (R // 4), R // 4)
        return held.at[sector, rows, pl.ds(pl.multiple_of(c * Q, 128), Q)]

    pieces = [(d, j) for j in range(4 * K) for d in range(1, S)]

    def y_copy(d, j, source):
        ref = part(near, source, j, cm)
        return remote(ref, ref, g_send.at[d - 1, j], g_recv.at[d - 1, j], y_peer(d))

    def x_copy(d, j):
        ref = part(near, d, j, cm)
        return remote(ref, part(far, d, j, cm), h_send.at[d - 1, j], h_recv.at[d - 1, j], x_peer)

    def core_copy(d, j, held, c, n):
        ref = part(held, d, j, c)
        return remote(ref, ref, f_send.at[n, d - 1, j], f_recv.at[n, d - 1, j], core_peer)

    sent = []
    own_loads[0].wait()
    for d, j in pieces:
        cp = y_copy(d, j, 0)
        cp.start()
        sent.append(cp)
    own_loads[1].wait()

    targets = [target_ref[t] for t in range(slots)]
    ranks = []
    for t in range(slots):
        rank = jnp.int32(0)
        for u in range(slots):
            ahead = targets[u] <= targets[t] if u < t else targets[u] < targets[t]
            if u != t:
                rank = rank + jnp.where(ahead, 1, 0)
        ranks.append(rank)
    before = jnp.int32(-1)
    for n in range(slots):
        slot, target = jnp.int32(0), jnp.int32(0)
        for t in range(slots):
            slot = jnp.where(ranks[t] == n, t, slot)
            target = jnp.where(ranks[t] == n, targets[t], target)
        order[n] = slot
        joins[n] = jnp.where(target == before, 1.0, 0.0)
        before = target
    prod[0] = jnp.zeros(prod.shape[1:], F32)
    for d, j in pieces:
        y_copy(d, j, d).wait_recv()
        for cp in (x_copy(d, j), core_copy(d, j, near, cm, 0)):
            cp.start()
            sent.append(cp)
    for cp in l_loads:
        cp.wait()
    for d, j in pieces:
        core_copy(d, j, near, co, 0).wait_recv()

    depth_ids = lax.broadcasted_iota(jnp.int32, (1, R), 1)
    chunk = 4 if slots % 8 == 0 else 1

    def products(held, h, first, begin, end):
        def one(n):
            t = order[n]
            source = source_ref[t]
            limit = jnp.where(t < live_ref[0], rows_ref[source], 0)
            keep = jnp.where(depth_ids < limit, 1.0, 0.0).astype(BF16)
            lmat = lbuf[t].reshape(R, R) * keep
            half = jnp.dot(lmat, held[source], preferred_element_type=F32).astype(BF16)
            return lax.dot_general(
                half,
                rbuf[h, t],
                (((1,), (1,)), ((), ())),
                preferred_element_type=F32,
            )

        @pl.loop(begin // chunk, end // chunk)
        def _(m):
            for u in range(chunk):
                n = m * chunk + u
                total = one(n)
                if not first:
                    total = total + prod[n + 1] + prod[n] * joins[n]
                prod[n + 1] = total

    def sums(c, store):
        @pl.loop(0, S * K * Z * X)
        def _(m):
            s = m // (Z * X)
            zx = m % (Z * X)
            y, k = s // K, s % K
            z, x = zx // X, zx % X
            rows = pl.ds(pl.multiple_of((c * Z * X + zx) * B, B), B)
            upto = jnp.int32(0)
            below = jnp.int32(0)
            for t in range(slots):
                upto = upto + jnp.where(target_ref[t] <= s, 1, 0)
                below = below + jnp.where(target_ref[t] < s, 1, 0)
            store(y, k, z, x, prod[upto, rows, :] * jnp.where(upto > below, 1.0, 0.0))

    def store_send(y, k, z, x, total):
        for i in range(2):
            snd_a0[i, x, y, z, k] = total[:, 2 * i * Q : (2 * i + 1) * Q].astype(BF16)
            snd_b0[i, y, x, z, k] = total[:, (2 * i + 1) * Q : (2 * i + 2) * Q].astype(BF16)

    def store_own(y, k, z, x, total):
        for i in range(2):
            acc_a[i, x, y, z, k] = total[:, 2 * i * Q : (2 * i + 1) * Q]
            acc_b[i, y, x, z, k] = total[:, (2 * i + 1) * Q : (2 * i + 2) * Q]

    products(near, xm, True, 0, slots // 2)
    for d, j in pieces:
        x_copy(d, j).wait_recv()
        cp = core_copy(d, j, far, cm, 1)
        cp.start()
        sent.append(cp)
    products(near, xm, True, slots // 2, slots)
    for d, j in pieces:
        core_copy(d, j, far, co, 1).wait_recv()
    products(far, xo, False, 0, slots)
    sums(co, store_send)
    a0, b0 = [], []
    for i in range(2):
        a0.append(remote(snd_a0.at[i], rcv_a0.at[i], s0.at[0, i], r0.at[0, i], core_peer))
        b0.append(remote(snd_b0.at[i], rcv_b0.at[i], s0.at[1, i], r0.at[1, i], core_peer))
        a0[i].start()
        b0[i].start()
    sums(cm, store_own)

    a1, b1 = [], [[], []]
    for i in range(2):
        a0[i].wait_recv()
        snd_a1[i] = (acc_a[i, xo] + rcv_a0[i, xo].astype(F32)).astype(BF16)
        cp = remote(snd_a1.at[i], rcv_a1.at[i], sx.at[0, i], rx.at[0, i], x_peer)
        cp.start()
        a1.append(cp)
        b0[i].wait_recv()
        for d in range(1, S):
            yo = lax.rem(ym + d, S)
            snd_b1[i, d - 1] = (acc_b[i, yo] + rcv_b0[i, yo].astype(F32)).astype(BF16)
            cp = remote(
                snd_b1.at[i, d - 1],
                rcv_b1.at[i, d - 1],
                sy_b.at[i, d - 1],
                ry_b.at[i, d - 1],
                y_peer(d),
            )
            cp.start()
            b1[i].append(cp)

    def b_sum(i, x):
        total = acc_b[i, ym, x] + rcv_b0[i, ym, x].astype(F32)
        for d in range(1, S):
            total = total + rcv_b1[i, d - 1, x].astype(F32)
        return total

    a2, b2 = [[], []], []
    for i in range(2):
        a1[i].wait_recv()
        for d in range(1, S):
            yo = lax.rem(ym + d, S)
            snd_a2[i, d - 1] = (
                acc_a[i, xm, yo] + rcv_a0[i, xm, yo].astype(F32) + rcv_a1[i, yo].astype(F32)
            ).astype(BF16)
            cp = remote(
                snd_a2.at[i, d - 1],
                rcv_a2.at[i, d - 1],
                sy_a.at[i, d - 1],
                ry_a.at[i, d - 1],
                y_peer(d),
            )
            cp.start()
            a2[i].append(cp)
        for cp in b1[i]:
            cp.wait_recv()
        snd_b2[i] = b_sum(i, xo).astype(BF16)
        cp = remote(snd_b2.at[i], rcv_b2.at[i], sx.at[1, i], rx.at[1, i], x_peer)
        cp.start()
        b2.append(cp)

    def a_last(i, z):
        total = (
            acc_a[i, xm, ym, z]
            + rcv_a0[i, xm, ym, z].astype(F32)
            + rcv_a1[i, ym, z].astype(F32)
        )
        for d in range(1, S):
            total = total + rcv_a2[i, d - 1, z].astype(F32)
        return total

    def b_last(i, z):
        total = acc_b[i, ym, xm, z] + rcv_b0[i, ym, xm, z].astype(F32)
        for d in range(1, S):
            total = total + rcv_b1[i, d - 1, xm, z].astype(F32)
        return total + rcv_b2[i, z].astype(F32)

    z3 = []
    far_first = sorted(range(1, Z), key=lambda d: -min(d, Z - d))
    for i in range(2):
        for cp in a2[i]:
            cp.wait_recv()
        for n, own, snd, rcv in ((0, a_last, snd_a3, rcv_a3), (1, b_last, snd_b3, rcv_b3)):
            if n == 1:
                b2[i].wait_recv()
            copies = {}
            for d in far_first:
                snd[i, d - 1] = own(i, lax.rem(zm + d, Z)).astype(BF16)
                cp = remote(
                    snd.at[i, d - 1],
                    rcv.at[i, d - 1],
                    sz.at[n, i, d - 1],
                    rz.at[n, i, d - 1],
                    z_peer(d),
                )
                cp.start()
                copies[d] = cp
            z3.append((i, n, own, rcv, copies))

    ids = term * B + lax.broadcasted_iota(jnp.int32, (B, Q), 0)
    for i, n, own, rcv, copies in z3:
        total = own(i, zm)
        for d in range(1, Z):
            copies[d].wait_recv()
            total = total + rcv[i, d - 1].astype(F32)
            sent.append(copies[d])
        col = (2 * i + n) * Q
        for k in range(K):
            used = ids < rows_ref[ym * K + k]
            out[k, :, col : col + Q] = jnp.where(used, total[k], 0.0)

    sent += a0 + b0 + a1 + b2 + b1[0] + b1[1] + a2[0] + a2[1]
    for cp in sent:
        cp.wait_send()


def local(mesh_sizes, wave, left, right, source, target, live, sector_rows):
    T, S = mesh_sizes
    X = 2
    Z = T // (2 * X)
    K, R, C = wave.shape
    B = R // T
    H, Q = C // 2, C // 4
    slots = left.shape[0]
    dims = (Z, X, S, K, B, C)
    left = left.reshape(slots, Z * X, 2, B, R)
    vm = pltpu.VMEM
    dma = pltpu.SemaphoreType.DMA
    full_a = (2, X, S, Z, K, B, Q)
    full_b = (2, S, X, Z, K, B, Q)
    after_x = (2, S, Z, K, B, Q)
    after_y = (2, S - 1, X, Z, K, B, Q)
    both = (2, Z, K, B, Q)
    after_y2 = (2, S - 1, Z, K, B, Q)
    last = (2, Z - 1, K, B, Q)
    scratch = [
        vm((S * K, R, H), BF16),
        vm((S * K, R, H), BF16),
        vm((slots, 2, Z * X, B, R), BF16),
        vm((2, slots, C, H), BF16),
        vm((slots + 1, R, C), F32),
        vm(full_a, BF16),
        vm(full_b, BF16),
        vm(full_a, BF16),
        vm(full_b, BF16),
        vm(full_a, F32),
        vm(full_b, F32),
        vm(after_x, BF16),
        vm(after_x, BF16),
        vm(after_y, BF16),
        vm(after_y, BF16),
        vm(after_y2, BF16),
        vm(after_y2, BF16),
        vm(both, BF16),
        vm(both, BF16),
        vm(last, BF16),
        vm(last, BF16),
        vm(last, BF16),
        vm(last, BF16),
        pltpu.SMEM((slots,), jnp.int32),
        pltpu.SMEM((slots,), F32),
        dma((6,)),
        dma((S - 1, 4 * K)),
        dma((S - 1, 4 * K)),
        dma((S - 1, 4 * K)),
        dma((S - 1, 4 * K)),
        dma((2, S - 1, 4 * K)),
        dma((2, S - 1, 4 * K)),
        dma((2, 2)),
        dma((2, 2)),
        dma((2, 2)),
        dma((2, 2)),
        dma((2, S - 1)),
        dma((2, S - 1)),
        dma((2, S - 1)),
        dma((2, S - 1)),
        dma((2, 2, Z - 1)),
        dma((2, 2, Z - 1)),
    ]
    any_spec = pl.BlockSpec(memory_space=pl.ANY)
    smem = pl.BlockSpec(memory_space=pltpu.SMEM)
    return pl.pallas_call(
        functools.partial(kernel, dims),
        out_shape=jax.ShapeDtypeStruct((K, B, C), F32),
        in_specs=[any_spec] * 3 + [smem] * 4,
        out_specs=pl.BlockSpec(memory_space=pltpu.VMEM),
        scratch_shapes=scratch,
        compiler_params=pltpu.CompilerParams(
            collective_id=0, has_side_effects=True, vmem_limit_bytes=60 * 1024 * 1024
        ),
    )(wave, left, right, source, target, live, sector_rows)


def solution(mesh):
    in_specs = (
        P("sector", None, None),
        P(("term", "sector"), None, None),
        P(("term", "sector"), None, None),
        P(("term", "sector")),
        P(("term", "sector")),
        P(("term", "sector")),
        P(),
    )
    out_specs = P("sector", "term", None)
    sizes = (mesh.shape["term"], mesh.shape["sector"])
    return jax.shard_map(
        functools.partial(local, sizes),
        mesh=mesh,
        in_specs=in_specs,
        out_specs=out_specs,
        check_vma=False,
    )
```

profile of v0, /device:TPU:0, one launch (start us, length us, event | category | flops | bytes accessed | tf_op | source)
XLA Modules:
  0.0 43.9 jit_solution(8406140283481207721)
XLA Ops:
  0.7 41.6 %shard_map.73 = f32[2,32,512]{2,1,0:T(8,128)} custom-call(bf16[2,512,512]{2,1,0:T(8,128)(2,1)} %wave.1, bf16[8,8,2,32,512]{4,3,2,1,0:T(8,128)(2,1)} %bitcast.1, bf16[8,512,512]{2,1,0:T(8,128)(2,1)} %right.1, s32[8]{0:T(128)} %source_ref.1, s32[8]{0:T(128)} %target_ref.1, s32[1]{0:T(128)S(6)} %copy.9.live_ref, s32[4]{0:T(128)} %rows_ref.1), custom_call_target="tpu_custom_call" | custom-call | tf_op jit(solution)/shard_map/pallas_call | solution.py:426
  42.3 1.6 %copy.10 = f32[2,32,512]{2,1,0:T(8,128)} copy(f32[2,32,512]{2,1,0:T(8,128)} %shard_map.73) | data formatting | bytes 262144
where the time goes:
time: 44 us; the launch traced here: 43.9 us
  Pallas kernels  41.6 us (95%)
  local copies, waits for them, and re-layouts  1.57 us (4%)
  between operations  0.66 us (2%)
    pallas_call x1, Pallas kernels, local(): pl.pallas_call(functools.partial(kernel, dims), out_shape=jax.ShapeDtypeS...  41.6 us
    unnamed x1, local copies, waits for them, and re-layouts  1.57 us

commit v1 on v0

v1 whole, which is shorter than its diff:
```python
import functools

import jax
import jax.numpy as jnp
from jax import lax
from jax.experimental import pallas as pl
from jax.experimental.pallas import tpu as pltpu
from jax.sharding import PartitionSpec as P

BF16 = jnp.bfloat16
F32 = jnp.float32
STEPS = 8
RELAYED = 6
LAG = 8


def kernel(
    dims,
    wave,
    left,
    right,
    source_ref,
    target_ref,
    live_hbm,
    rows_ref,
    out,
    near,
    far,
    lbuf,
    rbuf,
    half,
    prod,
    snd_c,
    rcv_c,
    acc,
    snd_a1,
    rcv_a1,
    snd_b1,
    rcv_b1,
    snd_a2,
    rcv_a2,
    snd_b2,
    rcv_b2,
    snd_z,
    rcv_z,
    live_ref,
    order,
    joins,
    upto,
    has,
    load_sem,
    ready,
    g_send,
    g_recv,
    e_send,
    e_recv,
    h_send,
    h_recv,
    f_send,
    f_recv,
    c_send,
    c_recv,
    sa1,
    ra1,
    sb1,
    rb1,
    sa2,
    ra2,
    sb2,
    rb2,
    sz,
    rz,
):
    Z, X, S, K, B, C = dims
    H, Q = C // 2, C // 4
    R = wave.shape[1]
    M = R // X
    slots = left.shape[0]
    term = lax.axis_index("term")
    ym = lax.axis_index("sector")
    cm = lax.rem(term, 2)
    xm = lax.rem(term // 2, X)
    zm = term // (2 * X)
    co = 1 - cm
    xo = 1 - xm

    def dev(z, x, c, y):
        return ((z * X + x) * 2 + c, y)

    core_peer = dev(zm, xm, co, ym)
    x_peer = dev(zm, xo, cm, ym)

    def y_other(d):
        return lax.rem(ym + d, S)

    def y_peer(d):
        return dev(zm, xm, cm, y_other(d))

    def z_other(d):
        if Z & (Z - 1):
            return lax.rem(zm + d, Z)
        other, bit = zm, 1
        while bit < Z:
            if d & bit:
                other = other + bit * (1 - 2 * lax.rem(zm // bit, 2))
            bit *= 2
        return other

    def z_peer(d):
        return dev(z_other(d), xm, cm, ym)

    def remote(src, dst, ssem, rsem, peer):
        return pltpu.make_async_remote_copy(
            src_ref=src,
            dst_ref=dst,
            send_sem=ssem,
            recv_sem=rsem,
            device_id=peer,
            device_id_type=pl.DeviceIdType.MESH,
        )

    def signal(sem, peer):
        pl.semaphore_signal(sem, inc=1, device_id=peer, device_id_type=pl.DeviceIdType.MESH)

    barrier = pltpu.get_barrier_semaphore()
    z_sides = jnp.where(zm > 0, 1, 0) + jnp.where(zm < Z - 1, 1, 0)

    def signal_sides(sem):
        @pl.when(zm > 0)
        def _():
            signal(sem, dev(zm - 1, xm, cm, ym))

        @pl.when(zm < Z - 1)
        def _():
            signal(sem, dev(zm + 1, xm, cm, ym))

    direct = [core_peer, x_peer] + [y_peer(d) for d in range(1, S)]
    for peer in direct:
        signal(barrier, peer)
    signal_sides(barrier)

    mine = pl.ds(ym * K, K)

    def cols(x):
        return pl.ds(pl.multiple_of(x * H, 128), H)

    own_loads = [
        pltpu.make_async_copy(wave.at[:, :, cols(x)], held.at[mine], load_sem.at[n])
        for n, (x, held) in enumerate(((xm, near), (xo, far)))
    ]
    live_load = pltpu.make_async_copy(live_hbm, live_ref, load_sem.at[2])
    l_loads = [
        pltpu.make_async_copy(left.at[:, :, x, c], lbuf.at[:, x, c], load_sem.at[3 + 2 * x + c])
        for x in range(X)
        for c in range(2)
    ]
    r_loads = [
        pltpu.make_async_copy(
            right.at[:, :, cols(x)], rbuf.at[:, :, n * H : (n + 1) * H], load_sem.at[7 + n]
        )
        for n, x in enumerate((xm, xo))
    ]
    for cp in own_loads + [live_load] + l_loads + r_loads:
        cp.start()

    targets = [target_ref[t] for t in range(slots)]
    ranks = []
    for t in range(slots):
        rank = jnp.int32(0)
        for u in range(slots):
            ahead = targets[u] <= targets[t] if u < t else targets[u] < targets[t]
            if u != t:
                rank = rank + jnp.where(ahead, 1, 0)
        ranks.append(rank)
    before = jnp.int32(-1)
    for n in range(slots):
        slot, target = jnp.int32(0), jnp.int32(0)
        for t in range(slots):
            slot = jnp.where(ranks[t] == n, t, slot)
            target = jnp.where(ranks[t] == n, targets[t], target)
        order[n] = slot
        joins[n] = jnp.where(target == before, 1.0, 0.0)
        before = target
    for s in range(S * K):
        last, below = jnp.int32(0), jnp.int32(0)
        for t in range(slots):
            last = last + jnp.where(targets[t] <= s, 1, 0)
            below = below + jnp.where(targets[t] < s, 1, 0)
        upto[s] = last
        has[s] = jnp.where(last > below, 1.0, 0.0)
    prod[0] = jnp.zeros(prod.shape[1:], F32)
    live_load.wait()

    for cp in own_loads:
        cp.wait()
    pl.semaphore_wait(barrier, len(direct) + z_sides)
    if Z > 2:
        signal_sides(ready.at[0])

    step = R // STEPS
    tail = (STEPS - RELAYED) * step
    pieces = [(d, k, j) for k in range(K) for j in range(RELAYED) for d in range(1, S)]
    tails = [(d, k) for k in range(K) for d in range(1, S)]
    sent = []

    def begin(*copies):
        for cp in copies:
            cp.start()
            sent.append(cp)

    def part(held, d, k, j, c):
        sector = lax.rem(ym + S - d, S) * K + k
        rows = pl.ds(RELAYED * step, tail) if j == RELAYED else pl.ds(j * step, step)
        return held.at[sector, rows, pl.ds(pl.multiple_of(c * Q, 128), Q)]

    def y_copy(d, k, j, source):
        ref = part(near, source, k, j, cm)
        return remote(ref, ref, g_send.at[d - 1, k, j], g_recv.at[d - 1, k, j], y_peer(d))

    def y_far(d, k, source):
        ref = part(far, source, k, RELAYED, cm)
        return remote(ref, ref, e_send.at[d - 1, k], e_recv.at[d - 1, k], y_peer(d))

    def x_copy(d, k, j):
        ref = part(near, d, k, j, cm)
        dst = part(far, d, k, j, cm)
        return remote(ref, dst, h_send.at[d - 1, k, j], h_recv.at[d - 1, k, j], x_peer)

    def core_copy(d, k, j, n, c):
        ref = part((near, far)[n], d, k, j, c)
        return remote(ref, ref, f_send.at[n, d - 1, k, j], f_recv.at[n, d - 1, k, j], core_peer)

    for d, k, j in pieces:
        begin(y_copy(d, k, j, 0))
    for d, k in tails:
        begin(y_copy(d, k, RELAYED, 0))
    for d, k in tails:
        begin(y_far(d, k, 0))

    depth_ids = lax.broadcasted_iota(jnp.int32, (1, R), 1)
    chunk = 4 if slots % 4 == 0 else slots

    def first(n_held, x, g):
        held = (near, far)[n_held]
        for n in range(g * chunk, (g + 1) * chunk):
            t = order[n]
            source = source_ref[t]
            limit = jnp.where(t < live_ref[0], rows_ref[source], 0)
            keep = jnp.where(depth_ids < limit, 1.0, 0.0).astype(BF16)
            lmat = lbuf[t, x].reshape(M, R) * keep
            value = jnp.dot(lmat, held[source], preferred_element_type=F32).astype(BF16)
            half[n, x, :, n_held * H : (n_held + 1) * H] = value

    def second(i, x):
        for n in range(slots):
            total = lax.dot_general(
                half[n, x],
                rbuf[order[n], i * H : (i + 1) * H],
                (((1,), (1,)), ((), ())),
                preferred_element_type=F32,
            )
            prod[n + 1] = total.reshape(prod.shape[1:]) + prod[n] * joins[n]

    def core_send(i, xi):
        return remote(
            snd_c.at[i, xi], rcv_c.at[i, xi], c_send.at[i, xi], c_recv.at[i, xi], core_peer
        )

    def spread(i, xi):
        @pl.loop(0, S * K)
        def _(s):
            y, k = s // K, s % K
            away = prod[upto[s], co] * has[s]
            kept = prod[upto[s], cm] * has[s]
            for n in range(2):
                piece = slice(n * Q, (n + 1) * Q)
                snd_c[i, xi, n, y, k] = away[:, piece].astype(BF16).reshape(Z, B, Q)
                acc[i, xi, n, y, k] = kept[:, piece].reshape(Z, B, Q)

        begin(core_send(i, xi))

    handled = []

    def relay_far(count):
        for d, k, j in pieces[len(handled) : len(handled) + count]:
            x_copy(d, k, j).wait_recv()
            begin(core_copy(d, k, j, 1, cm))
            handled.append((d, k, j))

    for n, (d, k, j) in enumerate(pieces):
        y_copy(d, k, j, d).wait_recv()
        begin(x_copy(d, k, j), core_copy(d, k, j, 0, cm))
        if n >= LAG:
            relay_far(1)
    for d, k in tails:
        y_copy(d, k, RELAYED, d).wait_recv()
        begin(core_copy(d, k, RELAYED, 0, cm))
        relay_far(1)
    if Z > 2:
        pl.semaphore_wait(ready.at[0], z_sides)
        if Z > 3:
            signal_sides(ready.at[1])
    for cp in l_loads + r_loads:
        cp.wait()
    for d, k, j in pieces + [(d, k, RELAYED) for d, k in tails]:
        core_copy(d, k, j, 0, co).wait_recv()
    groups = slots // chunk
    work = [(x, g) for x in (xo, xm) for g in range(groups)]
    left_over = len(pieces) - len(handled)
    for n, (x, g) in enumerate(work):
        first(0, x, g)
        if n + 1 < len(work):
            relay_far(-(-left_over // (len(work) - 1)))
    relay_far(len(pieces))
    for d, k in tails:
        y_far(d, k, d).wait_recv()
        begin(core_copy(d, k, RELAYED, 1, cm))
    for d, k, j in pieces + [(d, k, RELAYED) for d, k in tails]:
        core_copy(d, k, j, 1, co).wait_recv()

    def base(i, xi, n, y):
        return acc[i, xi, n, y] + rcv_c[i, xi, n, y].astype(F32)

    def a1_copy(i, y):
        return remote(snd_a1.at[i, y], rcv_a1.at[i, y], sa1.at[i, y], ra1.at[i, y], x_peer)

    def b1_copy(i, xi, d):
        at = (i, xi, d - 1)
        return remote(snd_b1.at[at], rcv_b1.at[at], sb1.at[at], rb1.at[at], y_peer(d))

    def a2_copy(i, d):
        at = (i, d - 1)
        return remote(snd_a2.at[at], rcv_a2.at[at], sa2.at[at], ra2.at[at], y_peer(d))

    def b2_copy(i):
        return remote(snd_b2.at[i], rcv_b2.at[i], sb2.at[i], rb2.at[i], x_peer)

    def z_copy(i, n, d):
        at = (i, n, d - 1)
        return remote(snd_z.at[at], rcv_z.at[at], sz.at[at], rz.at[at], z_peer(d))

    def stage_one_away(i):
        core_send(i, 0).wait_recv()
        for d in range(1, S):
            yo = y_other(d)
            snd_a1[i, yo] = base(i, 0, 0, yo).astype(BF16)
            begin(a1_copy(i, yo))
            snd_b1[i, 0, d - 1] = base(i, 0, 1, yo).astype(BF16)
            begin(b1_copy(i, 0, d))
        snd_a1[i, ym] = base(i, 0, 0, ym).astype(BF16)
        begin(a1_copy(i, ym))

    def stage_one_kept(i):
        core_send(i, 1).wait_recv()
        for d in range(1, S):
            yo = y_other(d)
            snd_b1[i, 1, d - 1] = base(i, 1, 1, yo).astype(BF16)
            begin(b1_copy(i, 1, d))

    def stage_two(i):
        for d in range(1, S):
            yo = y_other(d)
            a1_copy(i, yo).wait_recv()
            snd_a2[i, d - 1] = (base(i, 1, 0, yo) + rcv_a1[i, yo].astype(F32)).astype(BF16)
            begin(a2_copy(i, d))
        total = base(i, 0, 1, ym)
        for d in range(1, S):
            b1_copy(i, 0, d).wait_recv()
            total = total + rcv_b1[i, 0, d - 1].astype(F32)
        snd_b2[i] = total.astype(BF16)
        begin(b2_copy(i))

    def z_own(i, n, z):
        total = acc[i, 1, n, ym, :, z] + rcv_c[i, 1, n, ym, :, z].astype(F32)
        if n == 0:
            total = total + rcv_a1[i, ym, :, z].astype(F32)
            for d in range(1, S):
                total = total + rcv_a2[i, d - 1, :, z].astype(F32)
        else:
            for d in range(1, S):
                total = total + rcv_b1[i, 1, d - 1, :, z].astype(F32)
            total = total + rcv_b2[i, :, z].astype(F32)
        return total

    def stage_three(i):
        for n in range(2):
            if n == 0:
                a1_copy(i, ym).wait_recv()
                for d in range(1, S):
                    a2_copy(i, d).wait_recv()
            else:
                for d in range(1, S):
                    b1_copy(i, 1, d).wait_recv()
                b2_copy(i).wait_recv()
            for d in range(Z - 1, 0, -1):
                snd_z[i, n, d - 1] = z_own(i, n, z_other(d)).astype(BF16)
                begin(z_copy(i, n, d))

    def first_far(x):
        for g in range(groups):
            first(1, x, g)

    first_far(xo)
    second(0, xo)
    spread(0, 0)
    first_far(xm)
    stage_one_away(0)
    second(0, xm)
    spread(0, 1)
    second(1, xo)
    spread(1, 0)
    stage_one_kept(0)
    second(1, xm)
    spread(1, 1)
    stage_one_away(1)
    stage_one_kept(1)
    stage_two(0)
    for p in range(1, Z - 2):
        pl.semaphore_wait(ready.at[p], z_sides)
        if p + 1 < Z - 2:
            signal_sides(ready.at[p + 1])
    stage_two(1)
    stage_three(0)
    stage_three(1)

    ids = term * B + lax.broadcasted_iota(jnp.int32, (B, Q), 0)
    for i in range(2):
        for n in range(2):
            total = z_own(i, n, zm)
            for d in range(Z - 1, 0, -1):
                z_copy(i, n, d).wait_recv()
                total = total + rcv_z[i, n, d - 1].astype(F32)
            col = (2 * i + n) * Q
            for k in range(K):
                used = ids < rows_ref[ym * K + k]
                out[k, :, col : col + Q] = jnp.where(used, total[k], 0.0)

    for cp in sent:
        cp.wait_send()


def local(mesh_sizes, wave, left, right, source, target, live, sector_rows):
    T, S = mesh_sizes
    X = 2
    Z = T // (2 * X)
    K, R, C = wave.shape
    B = R // T
    H, Q = C // 2, C // 4
    slots = left.shape[0]
    dims = (Z, X, S, K, B, C)
    left = left.reshape(slots, Z, X, 2, B, R)
    vm = pltpu.VMEM
    dma = pltpu.SemaphoreType.DMA
    share = (K, Z, B, Q)
    scratch = [
        vm((S * K, R, H), BF16),
        vm((S * K, R, H), BF16),
        vm((slots, X, 2, Z, B, R), BF16),
        vm((slots, C, C), BF16),
        vm((slots, X, R // X, C), BF16),
        vm((slots + 1, 2, Z * B, H), F32),
        vm((2, 2, 2, S) + share, BF16),
        vm((2, 2, 2, S) + share, BF16),
        vm((2, 2, 2, S) + share, F32),
        vm((2, S) + share, BF16),
        vm((2, S) + share, BF16),
        vm((2, 2, S - 1) + share, BF16),
        vm((2, 2, S - 1) + share, BF16),
        vm((2, S - 1) + share, BF16),
        vm((2, S - 1) + share, BF16),
        vm((2,) + share, BF16),
        vm((2,) + share, BF16),
        vm((2, 2, Z - 1, K, B, Q), BF16),
        vm((2, 2, Z - 1, K, B, Q), BF16),
        pltpu.SMEM((1,), jnp.int32),
        pltpu.SMEM((slots,), jnp.int32),
        pltpu.SMEM((slots,), F32),
        pltpu.SMEM((S * K,), jnp.int32),
        pltpu.SMEM((S * K,), F32),
        dma((9,)),
        pltpu.SemaphoreType.REGULAR((max(Z - 2, 1),)),
        dma((S - 1, K, RELAYED + 1)),
        dma((S - 1, K, RELAYED + 1)),
        dma((S - 1, K)),
        dma((S - 1, K)),
        dma((S - 1, K, RELAYED)),
        dma((S - 1, K, RELAYED)),
        dma((2, S - 1, K, RELAYED + 1)),
        dma((2, S - 1, K, RELAYED + 1)),
        dma((2, 2)),
        dma((2, 2)),
        dma((2, S)),
        dma((2, S)),
        dma((2, 2, S - 1)),
        dma((2, 2, S - 1)),
        dma((2, S - 1)),
        dma((2, S - 1)),
        dma((2,)),
        dma((2,)),
        dma((2, 2, Z - 1)),
        dma((2, 2, Z - 1)),
    ]
    any_spec = pl.BlockSpec(memory_space=pl.ANY)
    smem = pl.BlockSpec(memory_space=pltpu.SMEM)
    return pl.pallas_call(
        functools.partial(kernel, dims),
        out_shape=jax.ShapeDtypeStruct((K, B, C), F32),
        in_specs=[any_spec] * 3 + [smem] * 2 + [any_spec, smem],
        out_specs=pl.BlockSpec(memory_space=pltpu.VMEM),
        scratch_shapes=scratch,
        compiler_params=pltpu.CompilerParams(
            collective_id=0, has_side_effects=True, vmem_limit_bytes=60 * 1024 * 1024
        ),
    )(wave, left, right, source, target, live, sector_rows)


def solution(mesh):
    in_specs = (
        P("sector", None, None),
        P(("term", "sector"), None, None),
        P(("term", "sector"), None, None),
        P(("term", "sector")),
        P(("term", "sector")),
        P(("term", "sector")),
        P(),
    )
    out_specs = P("sector", "term", None)
    sizes = (mesh.shape["term"], mesh.shape["sector"])
    return jax.shard_map(
        functools.partial(local, sizes),
        mesh=mesh,
        in_specs=in_specs,
        out_specs=out_specs,
        check_vma=False,
    )
```

time: 44 us -> 41.6 us (0.945)
  Pallas kernels: 41.6 us -> 39.2 us
    pallas_call x1, Pallas kernels: 41.6 us -> 39.2 us  [local(): pl.pallas_call(functools.partial(kernel, dims), out_shape=jax.ShapeDtypeS...]
where the time goes in v1:
time: 41.6 us; the launch traced here: 41.4 us
  Pallas kernels  39.2 us (94%)
  local copies, waits for them, and re-layouts  1.57 us (4%)
  between operations  0.66 us (2%)
    pallas_call x1, Pallas kernels, local(): pl.pallas_call(functools.partial(kernel, dims), out_shape=jax.ShapeDtypeS...  39.2 us
    unnamed x1, local copies, waits for them, and re-layouts  1.57 us

profile of v1, /device:TPU:0, one launch (start us, length us, event | category | flops | bytes accessed | tf_op | source)
XLA Modules:
  0.0 41.4 jit_solution(16778898327985750926)
XLA Ops:
  0.7 39.2 %shard_map.73 = f32[2,32,512]{2,1,0:T(8,128)} custom-call(bf16[2,512,512]{2,1,0:T(8,128)(2,1)} %wave.1, bf16[8,4,2,2,32,512]{5,4,3,2,1,0:T(8,128)(2,1)} %bitcast.1, bf16[8,512,512]{2,1,0:T(8,128)(2,1)} %right.1, s32[8]{0:T(128)} %source_ref.1, s32[8]{0:T(128)} %target_ref.1, s32[1]{0:T(128)S(6)} %copy.9.live_hbm, s32[4]{0:T(128)} %rows_ref.1), custom_call_target="tpu_custom_call" | custom-call | tf_op jit(solution)/shard_map/pallas_call | solution.py:505
  39.8 1.6 %copy.10 = f32[2,32,512]{2,1,0:T(8,128)} copy(f32[2,32,512]{2,1,0:T(8,128)} %shard_map.73) | data formatting | bytes 262144

commit v2 on v1

--- a/solution.py
+++ b/solution.py
@@ -11,7 +11,7 @@
 F32 = jnp.float32
 STEPS = 8
 RELAYED = 6
-LAG = 8
+LAG = 7
 
 
 def kernel(
@@ -52,23 +52,15 @@
     ready,
     g_send,
     g_recv,
-    e_send,
     e_recv,
-    h_send,
     h_recv,
-    f_send,
     f_recv,
-    c_send,
+    r_send,
     c_recv,
-    sa1,
     ra1,
-    sb1,
     rb1,
-    sa2,
     ra2,
-    sb2,
     rb2,
-    sz,
     rz,
 ):
     Z, X, S, K, B, C = dims
@@ -150,13 +142,13 @@
     ]
     live_load = pltpu.make_async_copy(live_hbm, live_ref, load_sem.at[2])
     l_loads = [
-        pltpu.make_async_copy(left.at[:, :, x, c], lbuf.at[:, x, c], load_sem.at[3 + 2 * x + c])
+        pltpu.make_async_copy(left.at[:, :, x, c], lbuf.at[:, x, c], load_sem.at[3])
         for x in range(X)
         for c in range(2)
     ]
     r_loads = [
         pltpu.make_async_copy(
-            right.at[:, :, cols(x)], rbuf.at[:, :, n * H : (n + 1) * H], load_sem.at[7 + n]
+            right.at[:, :, cols(x)], rbuf.at[:, :, n * H : (n + 1) * H], load_sem.at[4]
         )
         for n, x in enumerate((xm, xo))
     ]
@@ -201,12 +193,10 @@
     tail = (STEPS - RELAYED) * step
     pieces = [(d, k, j) for k in range(K) for j in range(RELAYED) for d in range(1, S)]
     tails = [(d, k) for k in range(K) for d in range(1, S)]
-    sent = []
 
     def begin(*copies):
         for cp in copies:
             cp.start()
-            sent.append(cp)
 
     def part(held, d, k, j, c):
         sector = lax.rem(ym + S - d, S) * K + k
@@ -215,20 +205,20 @@
 
     def y_copy(d, k, j, source):
         ref = part(near, source, k, j, cm)
-        return remote(ref, ref, g_send.at[d - 1, k, j], g_recv.at[d - 1, k, j], y_peer(d))
+        return remote(ref, ref, g_send.at[0], g_recv.at[d - 1, k, j], y_peer(d))
 
     def y_far(d, k, source):
         ref = part(far, source, k, RELAYED, cm)
-        return remote(ref, ref, e_send.at[d - 1, k], e_recv.at[d - 1, k], y_peer(d))
+        return remote(ref, ref, g_send.at[1], e_recv.at[d - 1, k], y_peer(d))
 
     def x_copy(d, k, j):
         ref = part(near, d, k, j, cm)
         dst = part(far, d, k, j, cm)
-        return remote(ref, dst, h_send.at[d - 1, k, j], h_recv.at[d - 1, k, j], x_peer)
+        return remote(ref, dst, g_send.at[2], h_recv.at[d - 1, k, j], x_peer)
 
     def core_copy(d, k, j, n, c):
         ref = part((near, far)[n], d, k, j, c)
-        return remote(ref, ref, f_send.at[n, d - 1, k, j], f_recv.at[n, d - 1, k, j], core_peer)
+        return remote(ref, ref, g_send.at[3 + n], f_recv.at[n], core_peer)
 
     for d, k, j in pieces:
         begin(y_copy(d, k, j, 0))
@@ -263,7 +253,7 @@
 
     def core_send(i, xi):
         return remote(
-            snd_c.at[i, xi], rcv_c.at[i, xi], c_send.at[i, xi], c_recv.at[i, xi], core_peer
+            snd_c.at[i, xi], rcv_c.at[i, xi], r_send.at[0], c_recv.at[i, xi], core_peer
         )
 
     def spread(i, xi):
@@ -300,44 +290,43 @@
         pl.semaphore_wait(ready.at[0], z_sides)
         if Z > 3:
             signal_sides(ready.at[1])
-    for cp in l_loads + r_loads:
-        cp.wait()
-    for d, k, j in pieces + [(d, k, RELAYED) for d, k in tails]:
-        core_copy(d, k, j, 0, co).wait_recv()
-    groups = slots // chunk
-    work = [(x, g) for x in (xo, xm) for g in range(groups)]
-    left_over = len(pieces) - len(handled)
-    for n, (x, g) in enumerate(work):
-        first(0, x, g)
-        if n + 1 < len(work):
-            relay_far(-(-left_over // (len(work) - 1)))
     relay_far(len(pieces))
     for d, k in tails:
         y_far(d, k, d).wait_recv()
         begin(core_copy(d, k, RELAYED, 1, cm))
-    for d, k, j in pieces + [(d, k, RELAYED) for d, k in tails]:
-        core_copy(d, k, j, 1, co).wait_recv()
+    pltpu.make_async_copy(lbuf, lbuf, load_sem.at[3]).wait()
+    pltpu.make_async_copy(rbuf, rbuf, load_sem.at[4]).wait()
+    others = pl.ds(0, (S - 1) * K)
+
+    def shares(held, rows):
+        return held.at[others, rows, pl.ds(0, Q)]
+
+    whole, most, rest = pl.ds(0, R), pl.ds(0, RELAYED * step), pl.ds(0, tail)
+
+    def all_of(held, rows, ssem, rsem, peer):
+        return remote(shares(held, rows), shares(held, rows), ssem, rsem, peer)
 
     def base(i, xi, n, y):
         return acc[i, xi, n, y] + rcv_c[i, xi, n, y].astype(F32)
 
     def a1_copy(i, y):
-        return remote(snd_a1.at[i, y], rcv_a1.at[i, y], sa1.at[i, y], ra1.at[i, y], x_peer)
+        return remote(snd_a1.at[i, y], rcv_a1.at[i, y], r_send.at[1], ra1.at[i, y], x_peer)
 
     def b1_copy(i, xi, d):
         at = (i, xi, d - 1)
-        return remote(snd_b1.at[at], rcv_b1.at[at], sb1.at[at], rb1.at[at], y_peer(d))
-
-    def a2_copy(i, d):
-        at = (i, d - 1)
-        return remote(snd_a2.at[at], rcv_a2.at[at], sa2.at[at], ra2.at[at], y_peer(d))
-
-    def b2_copy(i):
-        return remote(snd_b2.at[i], rcv_b2.at[i], sb2.at[i], rb2.at[i], x_peer)
-
-    def z_copy(i, n, d):
-        at = (i, n, d - 1)
-        return remote(snd_z.at[at], rcv_z.at[at], sz.at[at], rz.at[at], z_peer(d))
+        return remote(snd_b1.at[at], rcv_b1.at[at], r_send.at[2], rb1.at[at], y_peer(d))
+
+    def a2_copy(i, d, k):
+        at = (i, d - 1, k)
+        return remote(snd_a2.at[at], rcv_a2.at[at], r_send.at[3], ra2.at[at], y_peer(d))
+
+    def b2_copy(i, k):
+        at = (i, k)
+        return remote(snd_b2.at[at], rcv_b2.at[at], r_send.at[4], rb2.at[at], x_peer)
+
+    def z_copy(i, n, k, d):
+        at = (i, n, k, d - 1)
+        return remote(snd_z.at[at], rcv_z.at[at], r_send.at[5], rz.at[i, n, k], z_peer(d))
 
     def stage_one_away(i):
         core_send(i, 0).wait_recv()
@@ -347,6 +336,8 @@
             begin(a1_copy(i, yo))
             snd_b1[i, 0, d - 1] = base(i, 0, 1, yo).astype(BF16)
             begin(b1_copy(i, 0, d))
+
+    def stage_one_own(i):
         snd_a1[i, ym] = base(i, 0, 0, ym).astype(BF16)
         begin(a1_copy(i, ym))
 
@@ -359,52 +350,62 @@
 
     def stage_two(i):
         for d in range(1, S):
-            yo = y_other(d)
-            a1_copy(i, yo).wait_recv()
-            snd_a2[i, d - 1] = (base(i, 1, 0, yo) + rcv_a1[i, yo].astype(F32)).astype(BF16)
-            begin(a2_copy(i, d))
-        total = base(i, 0, 1, ym)
+            a1_copy(i, y_other(d)).wait_recv()
         for d in range(1, S):
             b1_copy(i, 0, d).wait_recv()
-            total = total + rcv_b1[i, 0, d - 1].astype(F32)
-        snd_b2[i] = total.astype(BF16)
-        begin(b2_copy(i))
-
-    def z_own(i, n, z):
-        total = acc[i, 1, n, ym, :, z] + rcv_c[i, 1, n, ym, :, z].astype(F32)
+        for k in range(K):
+            for d in range(1, S):
+                yo = y_other(d)
+                total = acc[i, 1, 0, yo, k] + rcv_c[i, 1, 0, yo, k].astype(F32)
+                snd_a2[i, d - 1, k] = (total + rcv_a1[i, yo, k].astype(F32)).astype(BF16)
+                begin(a2_copy(i, d, k))
+            total = acc[i, 0, 1, ym, k] + rcv_c[i, 0, 1, ym, k].astype(F32)
+            for d in range(1, S):
+                total = total + rcv_b1[i, 0, d - 1, k].astype(F32)
+            snd_b2[i, k] = total.astype(BF16)
+            begin(b2_copy(i, k))
+
+    def z_own(i, n, k, z):
+        total = acc[i, 1, n, ym, k, z] + rcv_c[i, 1, n, ym, k, z].astype(F32)
         if n == 0:
-            total = total + rcv_a1[i, ym, :, z].astype(F32)
+            total = total + rcv_a1[i, ym, k, z].astype(F32)
             for d in range(1, S):
-                total = total + rcv_a2[i, d - 1, :, z].astype(F32)
+                total = total + rcv_a2[i, d - 1, k, z].astype(F32)
         else:
             for d in range(1, S):
-                total = total + rcv_b1[i, 1, d - 1, :, z].astype(F32)
-            total = total + rcv_b2[i, :, z].astype(F32)
+                total = total + rcv_b1[i, 1, d - 1, k, z].astype(F32)
+            total = total + rcv_b2[i, k, z].astype(F32)
         return total
 
     def stage_three(i):
-        for n in range(2):
-            if n == 0:
-                a1_copy(i, ym).wait_recv()
-                for d in range(1, S):
-                    a2_copy(i, d).wait_recv()
-            else:
-                for d in range(1, S):
-                    b1_copy(i, 1, d).wait_recv()
-                b2_copy(i).wait_recv()
-            for d in range(Z - 1, 0, -1):
-                snd_z[i, n, d - 1] = z_own(i, n, z_other(d)).astype(BF16)
-                begin(z_copy(i, n, d))
-
-    def first_far(x):
-        for g in range(groups):
-            first(1, x, g)
-
-    first_far(xo)
+        a1_copy(i, ym).wait_recv()
+        for d in range(1, S):
+            b1_copy(i, 1, d).wait_recv()
+        for k in range(K):
+            for n in range(2):
+                if n == 0:
+                    for d in range(1, S):
+                        a2_copy(i, d, k).wait_recv()
+                else:
+                    b2_copy(i, k).wait_recv()
+                for d in range(Z - 1, 0, -1):
+                    snd_z[i, n, k, d - 1] = z_own(i, n, k, z_other(d)).astype(BF16)
+                    begin(z_copy(i, n, k, d))
+
+    def first_all(n_held, x):
+        for g in range(slots // chunk):
+            first(n_held, x, g)
+
+    all_of(near, whole, g_send.at[3], f_recv.at[0], core_peer).wait_recv()
+    first_all(0, xo)
+    all_of(far, whole, g_send.at[4], f_recv.at[1], core_peer).wait_recv()
+    first_all(1, xo)
     second(0, xo)
     spread(0, 0)
-    first_far(xm)
+    first_all(0, xm)
+    first_all(1, xm)
     stage_one_away(0)
+    stage_one_own(0)
     second(0, xm)
     spread(0, 1)
     second(1, xo)
@@ -413,8 +414,9 @@
     second(1, xm)
     spread(1, 1)
     stage_one_away(1)
+    stage_two(0)
+    stage_one_own(1)
     stage_one_kept(1)
-    stage_two(0)
     for p in range(1, Z - 2):
         pl.semaphore_wait(ready.at[p], z_sides)
         if p + 1 < Z - 2:
@@ -425,18 +427,24 @@
 
     ids = term * B + lax.broadcasted_iota(jnp.int32, (B, Q), 0)
     for i in range(2):
-        for n in range(2):
-            total = z_own(i, n, zm)
-            for d in range(Z - 1, 0, -1):
-                z_copy(i, n, d).wait_recv()
-                total = total + rcv_z[i, n, d - 1].astype(F32)
-            col = (2 * i + n) * Q
-            for k in range(K):
-                used = ids < rows_ref[ym * K + k]
-                out[k, :, col : col + Q] = jnp.where(used, total[k], 0.0)
-
-    for cp in sent:
-        cp.wait_send()
+        for k in range(K):
+            used = ids < rows_ref[ym * K + k]
+            for n in range(2):
+                total = z_own(i, n, k, zm)
+                got = rcv_z.at[i, n, k]
+                remote(got, got, r_send.at[5], rz.at[i, n, k], core_peer).wait_recv()
+                for d in range(Z - 1, 0, -1):
+                    total = total + rcv_z[i, n, k, d - 1].astype(F32)
+                col = (2 * i + n) * Q
+                out[k, :, col : col + Q] = jnp.where(used, total, 0.0)
+
+    all_of(near, whole, g_send.at[0], f_recv.at[0], core_peer).wait_send()
+    all_of(far, rest, g_send.at[1], f_recv.at[0], core_peer).wait_send()
+    all_of(near, most, g_send.at[2], f_recv.at[0], core_peer).wait_send()
+    all_of(near, whole, g_send.at[3], f_recv.at[0], core_peer).wait_send()
+    all_of(far, whole, g_send.at[4], f_recv.at[0], core_peer).wait_send()
+    for n, ref in enumerate((snd_c, snd_a1, snd_b1, snd_a2, snd_b2, snd_z)):
+        remote(ref, ref, r_send.at[n], f_recv.at[0], core_peer).wait_send()
 
 
 def local(mesh_sizes, wave, left, right, source, target, live, sector_rows):
@@ -470,35 +478,27 @@
         vm((2, S - 1) + share, BF16),
         vm((2,) + share, BF16),
         vm((2,) + share, BF16),
-        vm((2, 2, Z - 1, K, B, Q), BF16),
-        vm((2, 2, Z - 1, K, B, Q), BF16),
+        vm((2, 2, K, Z - 1, B, Q), BF16),
+        vm((2, 2, K, Z - 1, B, Q), BF16),
         pltpu.SMEM((1,), jnp.int32),
         pltpu.SMEM((slots,), jnp.int32),
         pltpu.SMEM((slots,), F32),
         pltpu.SMEM((S * K,), jnp.int32),
         pltpu.SMEM((S * K,), F32),
-        dma((9,)),
+        dma((5,)),
         pltpu.SemaphoreType.REGULAR((max(Z - 2, 1),)),
-        dma((S - 1, K, RELAYED + 1)),
+        dma((5,)),
         dma((S - 1, K, RELAYED + 1)),
         dma((S - 1, K)),
-        dma((S - 1, K)),
         dma((S - 1, K, RELAYED)),
-        dma((S - 1, K, RELAYED)),
-        dma((2, S - 1, K, RELAYED + 1)),
-        dma((2, S - 1, K, RELAYED + 1)),
-        dma((2, 2)),
+        dma((2,)),
+        dma((6,)),
         dma((2, 2)),
         dma((2, S)),
-        dma((2, S)),
         dma((2, 2, S - 1)),
-        dma((2, 2, S - 1)),
-        dma((2, S - 1)),
-        dma((2, S - 1)),
-        dma((2,)),
-        dma((2,)),
-        dma((2, 2, Z - 1)),
-        dma((2, 2, Z - 1)),
+        dma((2, S - 1, K)),
+        dma((2, K)),
+        dma((2, 2, K)),
     ]
     any_spec = pl.BlockSpec(memory_space=pl.ANY)
     smem = pl.BlockSpec(memory_space=pltpu.SMEM)

time: 41.6 us -> 38.1 us (0.916)
  Pallas kernels: 39.2 us -> 35.7 us
    pallas_call x1, Pallas kernels: 39.2 us -> 35.7 us  [local(): pl.pallas_call(functools.partial(kernel, dims), out_shape=jax.ShapeDtypeS...]
where the time goes in v2:
time: 38.1 us; the launch traced here: 37.9 us
  Pallas kernels  35.7 us (94%)
  local copies, waits for them, and re-layouts  1.57 us (4%)
  between operations  0.66 us (2%)
    pallas_call x1, Pallas kernels, local(): pl.pallas_call(functools.partial(kernel, dims), out_shape=jax.ShapeDtypeS...  35.7 us
    unnamed x1, local copies, waits for them, and re-layouts  1.57 us

profile of v2, /device:TPU:0, one launch (start us, length us, event | category | flops | bytes accessed | tf_op | source)
XLA Modules:
  0.0 37.9 jit_solution(2672839867731232974)
XLA Ops:
  0.7 35.7 %shard_map.73 = f32[2,32,512]{2,1,0:T(8,128)} custom-call(bf16[2,512,512]{2,1,0:T(8,128)(2,1)} %wave.1, bf16[8,4,2,2,32,512]{5,4,3,2,1,0:T(8,128)(2,1)} %bitcast.1, bf16[8,512,512]{2,1,0:T(8,128)(2,1)} %right.1, s32[8]{0:T(128)} %source_ref.1, s32[8]{0:T(128)} %target_ref.1, s32[1]{0:T(128)S(6)} %copy.9.live_hbm, s32[4]{0:T(128)} %rows_ref.1), custom_call_target="tpu_custom_call" | custom-call | tf_op jit(solution)/shard_map/pallas_call | solution.py:505
  36.4 1.6 %copy.10 = f32[2,32,512]{2,1,0:T(8,128)} copy(f32[2,32,512]{2,1,0:T(8,128)} %shard_map.73) | data formatting | bytes 262144

commit v3 on v2

--- a/solution.py
+++ b/solution.py
@@ -10,8 +10,8 @@
 BF16 = jnp.bfloat16
 F32 = jnp.float32
 STEPS = 8
-RELAYED = 6
-LAG = 7
+RELAYED = 5
+LAG = 8
 
 
 def kernel(
@@ -19,10 +19,7 @@
     wave,
     left,
     right,
-    source_ref,
-    target_ref,
-    live_hbm,
-    rows_ref,
+    packed,
     out,
     near,
     far,
@@ -43,7 +40,6 @@
     rcv_b2,
     snd_z,
     rcv_z,
-    live_ref,
     order,
     joins,
     upto,
@@ -140,7 +136,6 @@
         pltpu.make_async_copy(wave.at[:, :, cols(x)], held.at[mine], load_sem.at[n])
         for n, (x, held) in enumerate(((xm, near), (xo, far)))
     ]
-    live_load = pltpu.make_async_copy(live_hbm, live_ref, load_sem.at[2])
     l_loads = [
         pltpu.make_async_copy(left.at[:, :, x, c], lbuf.at[:, x, c], load_sem.at[3])
         for x in range(X)
@@ -152,10 +147,10 @@
         )
         for n, x in enumerate((xm, xo))
     ]
-    for cp in own_loads + [live_load] + l_loads + r_loads:
+    for cp in own_loads + l_loads + r_loads:
         cp.start()
 
-    targets = [target_ref[t] for t in range(slots)]
+    targets = [packed[slots + t] for t in range(slots)]
     ranks = []
     for t in range(slots):
         rank = jnp.int32(0)
@@ -181,7 +176,6 @@
         upto[s] = last
         has[s] = jnp.where(last > below, 1.0, 0.0)
     prod[0] = jnp.zeros(prod.shape[1:], F32)
-    live_load.wait()
 
     for cp in own_loads:
         cp.wait()
@@ -234,8 +228,8 @@
         held = (near, far)[n_held]
         for n in range(g * chunk, (g + 1) * chunk):
             t = order[n]
-            source = source_ref[t]
-            limit = jnp.where(t < live_ref[0], rows_ref[source], 0)
+            source = packed[t]
+            limit = jnp.where(t < packed[2 * slots], packed[2 * slots + 1 + source], 0)
             keep = jnp.where(depth_ids < limit, 1.0, 0.0).astype(BF16)
             lmat = lbuf[t, x].reshape(M, R) * keep
             value = jnp.dot(lmat, held[source], preferred_element_type=F32).astype(BF16)
@@ -428,7 +422,7 @@
     ids = term * B + lax.broadcasted_iota(jnp.int32, (B, Q), 0)
     for i in range(2):
         for k in range(K):
-            used = ids < rows_ref[ym * K + k]
+            used = ids < packed[2 * slots + 1 + ym * K + k]
             for n in range(2):
                 total = z_own(i, n, k, zm)
                 got = rcv_z.at[i, n, k]
@@ -480,7 +474,6 @@
         vm((2,) + share, BF16),
         vm((2, 2, K, Z - 1, B, Q), BF16),
         vm((2, 2, K, Z - 1, B, Q), BF16),
-        pltpu.SMEM((1,), jnp.int32),
         pltpu.SMEM((slots,), jnp.int32),
         pltpu.SMEM((slots,), F32),
         pltpu.SMEM((S * K,), jnp.int32),
@@ -505,13 +498,13 @@
     return pl.pallas_call(
         functools.partial(kernel, dims),
         out_shape=jax.ShapeDtypeStruct((K, B, C), F32),
-        in_specs=[any_spec] * 3 + [smem] * 2 + [any_spec, smem],
+        in_specs=[any_spec] * 3 + [smem],
         out_specs=pl.BlockSpec(memory_space=pltpu.VMEM),
         scratch_shapes=scratch,
         compiler_params=pltpu.CompilerParams(
-            collective_id=0, has_side_effects=True, vmem_limit_bytes=60 * 1024 * 1024
+            collective_id=0, has_side_effects=True, vmem_limit_bytes=54784 * 1024
         ),
-    )(wave, left, right, source, target, live, sector_rows)
+    )(wave, left, right, jnp.concatenate([source, target, live, sector_rows]))
 
 
 def solution(mesh):

time: 38.1 us -> 36.5 us (0.958)
  Pallas kernels: 35.7 us -> 34.2 us
  local copies, waits for them, and re-layouts: 1.57 us -> 0.66 us
  other arithmetic: 0 us -> 0.77 us
    pallas_call x1, Pallas kernels: 35.7 us -> 34.2 us  [local(): pl.pallas_call(functools.partial(kernel, dims), out_shape=jax.ShapeDtypeS...]
    unnamed x1, local copies, waits for them, and re-layouts: 1.57 us -> 0.66 us
    concatenate x0 -> x1, other arithmetic: none -> 0.77 us  [local(): jnp.concatenate([source, target, live, sector_rows])]
where the time goes in v3:
time: 36.5 us; the launch traced here: 36.3 us
  Pallas kernels  34.2 us (94%)
  other arithmetic  0.77 us (2%)
  local copies, waits for them, and re-layouts  0.66 us (2%)
  between operations  0.66 us (2%)
    pallas_call x1, Pallas kernels, local(): pl.pallas_call(functools.partial(kernel, dims), out_shape=jax.ShapeDtypeS...  34.2 us
    concatenate x1, other arithmetic, local(): jnp.concatenate([source, target, live, sector_rows])  0.77 us

profile of v3, /device:TPU:0, one launch (start us, length us, event | category | flops | bytes accessed | tf_op | source)
XLA Modules:
  0.0 36.3 jit_solution(1627429700700094632)
XLA Ops:
  0.7 0.8 %pad_add_fusion.packed = s32[21]{0:T(128)S(1)} fusion(s32[4]{0:T(128)} %param.13, s32[1]{0:T(128)S(6)} %copy.9, s32[8]{0:T(128)} %param.11, s32[8]{0:T(128)} %param.10), kind=kLoop, calls=%fused_computation | loop fusion | flops 63 | bytes 168 | tf_op jit(solution)/shard_map/concatenate | solution.py:507
  1.4 34.2 %shard_map.73 = f32[2,32,512]{2,1,0:T(8,128)S(1)} custom-call(bf16[2,512,512]{2,1,0:T(8,128)(2,1)} %wave.1, bf16[8,4,2,2,32,512]{5,4,3,2,1,0:T(8,128)(2,1)} %bitcast.1, bf16[8,512,512]{2,1,0:T(8,128)(2,1)} %right.1, s32[21]{0:T(128)S(1)} %pad_add_fusion.packed), custom_call_target="tpu_custom_call" | custom-call | tf_op jit(solution)/shard_map/pallas_call | solution.py:498
  35.7 0.7 %copy.10 = f32[2,32,512]{2,1,0:T(8,128)} copy(f32[2,32,512]{2,1,0:T(8,128)S(1)} %shard_map.73) | data formatting | bytes 262144

commit v4 on v3

--- a/solution.py
+++ b/solution.py
@@ -52,6 +52,7 @@
     h_recv,
     f_recv,
     r_send,
+    z_send,
     c_recv,
     ra1,
     rb1,
@@ -62,7 +63,8 @@
     Z, X, S, K, B, C = dims
     H, Q = C // 2, C // 4
     R = wave.shape[1]
-    M = R // X
+    M = R // 2
+    Z2 = Z // 2
     slots = left.shape[0]
     term = lax.axis_index("term")
     ym = lax.axis_index("sector")
@@ -137,7 +139,8 @@
         for n, (x, held) in enumerate(((xm, near), (xo, far)))
     ]
     l_loads = [
-        pltpu.make_async_copy(left.at[:, :, x, c], lbuf.at[:, x, c], load_sem.at[3])
+        pltpu.make_async_copy(left.at[:, zh, :, x, c], lbuf.at[:, zh, c, x], load_sem.at[3])
+        for zh in range(2)
         for x in range(X)
         for c in range(2)
     ]
@@ -224,44 +227,42 @@
     depth_ids = lax.broadcasted_iota(jnp.int32, (1, R), 1)
     chunk = 4 if slots % 4 == 0 else slots
 
-    def first(n_held, x, g):
+    def first(n_held, zh, g):
         held = (near, far)[n_held]
         for n in range(g * chunk, (g + 1) * chunk):
             t = order[n]
             source = packed[t]
             limit = jnp.where(t < packed[2 * slots], packed[2 * slots + 1 + source], 0)
             keep = jnp.where(depth_ids < limit, 1.0, 0.0).astype(BF16)
-            lmat = lbuf[t, x].reshape(M, R) * keep
+            lmat = lbuf[t, zh].reshape(M, R) * keep
             value = jnp.dot(lmat, held[source], preferred_element_type=F32).astype(BF16)
-            half[n, x, :, n_held * H : (n_held + 1) * H] = value
-
-    def second(i, x):
+            half[n, zh, :, n_held * H : (n_held + 1) * H] = value
+
+    def second(zh, w):
         for n in range(slots):
             total = lax.dot_general(
-                half[n, x],
-                rbuf[order[n], i * H : (i + 1) * H],
+                half[n, zh],
+                rbuf[order[n], w * H : (w + 1) * H],
                 (((1,), (1,)), ((), ())),
                 preferred_element_type=F32,
             )
             prod[n + 1] = total.reshape(prod.shape[1:]) + prod[n] * joins[n]
 
-    def core_send(i, xi):
+    def core_send(zh, w):
         return remote(
-            snd_c.at[i, xi], rcv_c.at[i, xi], r_send.at[0], c_recv.at[i, xi], core_peer
+            snd_c.at[zh, w], rcv_c.at[zh, w], r_send.at[0], c_recv.at[zh, w], core_peer
         )
 
-    def spread(i, xi):
+    def spread(zh, w):
         @pl.loop(0, S * K)
         def _(s):
             y, k = s // K, s % K
             away = prod[upto[s], co] * has[s]
             kept = prod[upto[s], cm] * has[s]
-            for n in range(2):
-                piece = slice(n * Q, (n + 1) * Q)
-                snd_c[i, xi, n, y, k] = away[:, piece].astype(BF16).reshape(Z, B, Q)
-                acc[i, xi, n, y, k] = kept[:, piece].reshape(Z, B, Q)
-
-        begin(core_send(i, xi))
+            snd_c[zh, w, y, k] = away.astype(BF16).reshape(X, Z2, B, H)
+            acc[zh, w, y, k] = kept.reshape(X, Z2, B, H)
+
+        begin(core_send(zh, w))
 
     handled = []
 
@@ -300,145 +301,159 @@
     def all_of(held, rows, ssem, rsem, peer):
         return remote(shares(held, rows), shares(held, rows), ssem, rsem, peer)
 
-    def base(i, xi, n, y):
-        return acc[i, xi, n, y] + rcv_c[i, xi, n, y].astype(F32)
-
-    def a1_copy(i, y):
-        return remote(snd_a1.at[i, y], rcv_a1.at[i, y], r_send.at[1], ra1.at[i, y], x_peer)
-
-    def b1_copy(i, xi, d):
-        at = (i, xi, d - 1)
+    def base(zh, w, y, k, x):
+        return acc[zh, w, y, k, x] + rcv_c[zh, w, y, k, x].astype(F32)
+
+    def a1_copy(zh, y):
+        at = (zh, y)
+        return remote(snd_a1.at[at], rcv_a1.at[at], r_send.at[1], ra1.at[at], x_peer)
+
+    def b1_copy(zh, away, d):
+        at = (zh, away, d - 1)
         return remote(snd_b1.at[at], rcv_b1.at[at], r_send.at[2], rb1.at[at], y_peer(d))
 
-    def a2_copy(i, d, k):
-        at = (i, d - 1, k)
+    def a2_copy(zh, d, k):
+        at = (zh, d - 1, k)
         return remote(snd_a2.at[at], rcv_a2.at[at], r_send.at[3], ra2.at[at], y_peer(d))
 
-    def b2_copy(i, k):
-        at = (i, k)
+    def b2_copy(zh, k):
+        at = (zh, k)
         return remote(snd_b2.at[at], rcv_b2.at[at], r_send.at[4], rb2.at[at], x_peer)
 
-    def z_copy(i, n, k, d):
-        at = (i, n, k, d - 1)
-        return remote(snd_z.at[at], rcv_z.at[at], r_send.at[5], rz.at[i, n, k], z_peer(d))
-
-    def stage_one_away(i):
-        core_send(i, 0).wait_recv()
+    def z_copy(zh, w, k, i):
+        z = zh * Z2 + i
+        slot = lax.rem(zm - z - 1 + 2 * Z, Z)
+        return remote(
+            snd_z.at[zh, w, k, i],
+            rcv_z.at[w, k, slot],
+            z_send.at[zh, w, k, i],
+            rz.at[w, k],
+            dev(z, xm, cm, ym),
+        )
+
+    def stage_one_a(zh):
+        core_send(zh, 0).wait_recv()
+        for d in list(range(1, S)) + [0]:
+            y = y_other(d)
+            for k in range(K):
+                snd_a1[zh, y, k] = base(zh, 0, y, k, xo).astype(BF16)
+            begin(a1_copy(zh, y))
+
+    def stage_one_b(zh):
+        core_send(zh, 1).wait_recv()
+        for away, x in ((0, xo), (1, xm)):
+            for d in range(1, S):
+                for k in range(K):
+                    snd_b1[zh, away, d - 1, k] = base(zh, 1, y_other(d), k, x).astype(BF16)
+                begin(b1_copy(zh, away, d))
+
+    def stage_two_a(zh):
         for d in range(1, S):
             yo = y_other(d)
-            snd_a1[i, yo] = base(i, 0, 0, yo).astype(BF16)
-            begin(a1_copy(i, yo))
-            snd_b1[i, 0, d - 1] = base(i, 0, 1, yo).astype(BF16)
-            begin(b1_copy(i, 0, d))
-
-    def stage_one_own(i):
-        snd_a1[i, ym] = base(i, 0, 0, ym).astype(BF16)
-        begin(a1_copy(i, ym))
-
-    def stage_one_kept(i):
-        core_send(i, 1).wait_recv()
+            a1_copy(zh, yo).wait_recv()
+            for k in range(K):
+                total = base(zh, 0, yo, k, xm) + rcv_a1[zh, yo, k].astype(F32)
+                snd_a2[zh, d - 1, k] = total.astype(BF16)
+                begin(a2_copy(zh, d, k))
+
+    def stage_two_b(zh):
         for d in range(1, S):
-            yo = y_other(d)
-            snd_b1[i, 1, d - 1] = base(i, 1, 1, yo).astype(BF16)
-            begin(b1_copy(i, 1, d))
-
-    def stage_two(i):
-        for d in range(1, S):
-            a1_copy(i, y_other(d)).wait_recv()
-        for d in range(1, S):
-            b1_copy(i, 0, d).wait_recv()
+            b1_copy(zh, 0, d).wait_recv()
         for k in range(K):
+            total = base(zh, 1, ym, k, xo)
             for d in range(1, S):
-                yo = y_other(d)
-                total = acc[i, 1, 0, yo, k] + rcv_c[i, 1, 0, yo, k].astype(F32)
-                snd_a2[i, d - 1, k] = (total + rcv_a1[i, yo, k].astype(F32)).astype(BF16)
-                begin(a2_copy(i, d, k))
-            total = acc[i, 0, 1, ym, k] + rcv_c[i, 0, 1, ym, k].astype(F32)
+                total = total + rcv_b1[zh, 0, d - 1, k].astype(F32)
+            snd_b2[zh, k] = total.astype(BF16)
+            begin(b2_copy(zh, k))
+
+    def z_own(zh, w, k, i):
+        total = acc[zh, w, ym, k, xm, i] + rcv_c[zh, w, ym, k, xm, i].astype(F32)
+        if w == 0:
+            total = total + rcv_a1[zh, ym, k, i].astype(F32)
             for d in range(1, S):
-                total = total + rcv_b1[i, 0, d - 1, k].astype(F32)
-            snd_b2[i, k] = total.astype(BF16)
-            begin(b2_copy(i, k))
-
-    def z_own(i, n, k, z):
-        total = acc[i, 1, n, ym, k, z] + rcv_c[i, 1, n, ym, k, z].astype(F32)
-        if n == 0:
-            total = total + rcv_a1[i, ym, k, z].astype(F32)
-            for d in range(1, S):
-                total = total + rcv_a2[i, d - 1, k, z].astype(F32)
+                total = total + rcv_a2[zh, d - 1, k, i].astype(F32)
         else:
             for d in range(1, S):
-                total = total + rcv_b1[i, 1, d - 1, k, z].astype(F32)
-            total = total + rcv_b2[i, k, z].astype(F32)
+                total = total + rcv_b1[zh, 1, d - 1, k, i].astype(F32)
+            total = total + rcv_b2[zh, k, i].astype(F32)
         return total
 
-    def stage_three(i):
-        a1_copy(i, ym).wait_recv()
+    def stage_three(zh):
+        a1_copy(zh, ym).wait_recv()
         for d in range(1, S):
-            b1_copy(i, 1, d).wait_recv()
+            b1_copy(zh, 1, d).wait_recv()
         for k in range(K):
-            for n in range(2):
-                if n == 0:
+            for w in range(2):
+                if w == 0:
                     for d in range(1, S):
-                        a2_copy(i, d, k).wait_recv()
+                        a2_copy(zh, d, k).wait_recv()
                 else:
-                    b2_copy(i, k).wait_recv()
-                for d in range(Z - 1, 0, -1):
-                    snd_z[i, n, k, d - 1] = z_own(i, n, k, z_other(d)).astype(BF16)
-                    begin(z_copy(i, n, k, d))
-
-    def first_all(n_held, x):
+                    b2_copy(zh, k).wait_recv()
+                for i in range(Z2):
+                    @pl.when(zm != zh * Z2 + i)
+                    def _():
+                        snd_z[zh, w, k, i] = z_own(zh, w, k, i).astype(BF16)
+                        begin(z_copy(zh, w, k, i))
+
+    def first_all(n_held, zh):
         for g in range(slots // chunk):
-            first(n_held, x, g)
+            first(n_held, zh, g)
 
     all_of(near, whole, g_send.at[3], f_recv.at[0], core_peer).wait_recv()
-    first_all(0, xo)
+    first_all(0, 0)
     all_of(far, whole, g_send.at[4], f_recv.at[1], core_peer).wait_recv()
-    first_all(1, xo)
-    second(0, xo)
+    first_all(1, 0)
+    second(0, 0)
     spread(0, 0)
-    first_all(0, xm)
-    first_all(1, xm)
-    stage_one_away(0)
-    stage_one_own(0)
-    second(0, xm)
+    second(0, 1)
     spread(0, 1)
-    second(1, xo)
+    stage_one_a(0)
+    first_all(0, 1)
+    stage_one_b(0)
+    first_all(1, 1)
+    second(1, 0)
     spread(1, 0)
-    stage_one_kept(0)
-    second(1, xm)
+    second(1, 1)
     spread(1, 1)
-    stage_one_away(1)
-    stage_two(0)
-    stage_one_own(1)
-    stage_one_kept(1)
+    stage_two_a(0)
+    stage_two_b(0)
+    stage_one_a(1)
+    stage_one_b(1)
     for p in range(1, Z - 2):
         pl.semaphore_wait(ready.at[p], z_sides)
         if p + 1 < Z - 2:
             signal_sides(ready.at[p + 1])
-    stage_two(1)
     stage_three(0)
+    stage_two_a(1)
+    stage_two_b(1)
     stage_three(1)
 
-    ids = term * B + lax.broadcasted_iota(jnp.int32, (B, Q), 0)
-    for i in range(2):
-        for k in range(K):
-            used = ids < packed[2 * slots + 1 + ym * K + k]
-            for n in range(2):
-                total = z_own(i, n, k, zm)
-                got = rcv_z.at[i, n, k]
-                remote(got, got, r_send.at[5], rz.at[i, n, k], core_peer).wait_recv()
-                for d in range(Z - 1, 0, -1):
-                    total = total + rcv_z[i, n, k, d - 1].astype(F32)
-                col = (2 * i + n) * Q
-                out[k, :, col : col + Q] = jnp.where(used, total, 0.0)
+    ids = term * B + lax.broadcasted_iota(jnp.int32, (B, H), 0)
+    my_half, my_place = zm // Z2, lax.rem(zm, Z2)
+    for k in range(K):
+        used = ids < packed[2 * slots + 1 + ym * K + k]
+        for w in range(2):
+            total = z_own(my_half, w, k, my_place)
+            got = rcv_z.at[w, k]
+            remote(got, got, r_send.at[0], rz.at[w, k], core_peer).wait_recv()
+            for n in range(Z - 1):
+                total = total + rcv_z[w, k, n].astype(F32)
+            out[k, :, w * H : (w + 1) * H] = jnp.where(used, total, 0.0)
 
     all_of(near, whole, g_send.at[0], f_recv.at[0], core_peer).wait_send()
     all_of(far, rest, g_send.at[1], f_recv.at[0], core_peer).wait_send()
     all_of(near, most, g_send.at[2], f_recv.at[0], core_peer).wait_send()
     all_of(near, whole, g_send.at[3], f_recv.at[0], core_peer).wait_send()
     all_of(far, whole, g_send.at[4], f_recv.at[0], core_peer).wait_send()
-    for n, ref in enumerate((snd_c, snd_a1, snd_b1, snd_a2, snd_b2, snd_z)):
+    for n, ref in enumerate((snd_c, snd_a1, snd_b1, snd_a2, snd_b2)):
         remote(ref, ref, r_send.at[n], f_recv.at[0], core_peer).wait_send()
+    for zh in range(2):
+        for i in range(Z2):
+            @pl.when(zm != zh * Z2 + i)
+            def _():
+                for w in range(2):
+                    for k in range(K):
+                        z_copy(zh, w, k, i).wait_send()
 
 
 def local(mesh_sizes, wave, left, right, source, target, live, sector_rows):
@@ -450,20 +465,21 @@
     H, Q = C // 2, C // 4
     slots = left.shape[0]
     dims = (Z, X, S, K, B, C)
-    left = left.reshape(slots, Z, X, 2, B, R)
+    left = left.reshape(slots, 2, Z // 2, X, 2, B, R)
     vm = pltpu.VMEM
     dma = pltpu.SemaphoreType.DMA
-    share = (K, Z, B, Q)
+    Z2 = Z // 2
+    share = (K, Z2, B, H)
     scratch = [
         vm((S * K, R, H), BF16),
         vm((S * K, R, H), BF16),
-        vm((slots, X, 2, Z, B, R), BF16),
+        vm((slots, 2, 2, X, Z2, B, R), BF16),
         vm((slots, C, C), BF16),
-        vm((slots, X, R // X, C), BF16),
-        vm((slots + 1, 2, Z * B, H), F32),
-        vm((2, 2, 2, S) + share, BF16),
-        vm((2, 2, 2, S) + share, BF16),
-        vm((2, 2, 2, S) + share, F32),
+        vm((slots, 2, R // 2, C), BF16),
+        vm((slots + 1, 2, X * Z2 * B, H), F32),
+        vm((2, 2, S, K, X, Z2, B, H), BF16),
+        vm((2, 2, S, K, X, Z2, B, H), BF16),
+        vm((2, 2, S, K, X, Z2, B, H), F32),
         vm((2, S) + share, BF16),
         vm((2, S) + share, BF16),
         vm((2, 2, S - 1) + share, BF16),
@@ -472,8 +488,8 @@
         vm((2, S - 1) + share, BF16),
         vm((2,) + share, BF16),
         vm((2,) + share, BF16),
-        vm((2, 2, K, Z - 1, B, Q), BF16),
-        vm((2, 2, K, Z - 1, B, Q), BF16),
+        vm((2, 2) + share, BF16),
+        vm((2, K, Z - 1, B, H), BF16),
         pltpu.SMEM((slots,), jnp.int32),
         pltpu.SMEM((slots,), F32),
         pltpu.SMEM((S * K,), jnp.int32),
@@ -485,13 +501,14 @@
         dma((S - 1, K)),
         dma((S - 1, K, RELAYED)),
         dma((2,)),
-        dma((6,)),
+        dma((5,)),
+        dma((2, 2, K, Z2)),
         dma((2, 2)),
         dma((2, S)),
         dma((2, 2, S - 1)),
         dma((2, S - 1, K)),
         dma((2, K)),
-        dma((2, 2, K)),
+        dma((2, K)),
     ]
     any_spec = pl.BlockSpec(memory_space=pl.ANY)
     smem = pl.BlockSpec(memory_space=pltpu.SMEM)

time: 36.5 us -> 35.4 us (0.970)
  the two profiles are of different devices: /device:TPU:0 before, /device:TPU:24 now
where the time goes in v4:
time: 35.4 us; the launch traced here: 35.2 us
  Pallas kernels  33.1 us (94%)
  other arithmetic  0.77 us (2%)
  local copies, waits for them, and re-layouts  0.66 us (2%)
  between operations  0.66 us (2%)
    pallas_call x1, Pallas kernels, local(): pl.pallas_call(functools.partial(kernel, dims), out_shape=jax.ShapeDtypeS...  33.1 us
    concatenate x1, other arithmetic, local(): jnp.concatenate([source, target, live, sector_rows])  0.77 us

profile of v4, /device:TPU:24, one launch (start us, length us, event | category | flops | bytes accessed | tf_op | source)
XLA Modules:
  0.0 35.2 jit_solution(10349606895982826862)
XLA Ops:
  0.7 0.8 %pad_add_fusion.packed = s32[21]{0:T(128)S(1)} fusion(s32[4]{0:T(128)} %param.13, s32[1]{0:T(128)S(6)} %copy.9, s32[8]{0:T(128)} %param.11, s32[8]{0:T(128)} %param.10), kind=kLoop, calls=%fused_computation | loop fusion | flops 63 | bytes 168 | tf_op jit(solution)/shard_map/concatenate | solution.py:524
  1.4 33.1 %shard_map.73 = f32[2,32,512]{2,1,0:T(8,128)S(1)} custom-call(bf16[2,512,512]{2,1,0:T(8,128)(2,1)} %wave.1, bf16[8,2,2,2,2,32,512]{6,5,4,3,2,1,0:T(8,128)(2,1)} %bitcast.1, bf16[8,512,512]{2,1,0:T(8,128)(2,1)} %right.1, s32[21]{0:T(128)S(1)} %pad_add_fusion.packed), custom_call_target="tpu_custom_call" | custom-call | tf_op jit(solution)/shard_map/pallas_call | solution.py:515
  34.6 0.7 %copy.10 = f32[2,32,512]{2,1,0:T(8,128)} copy(f32[2,32,512]{2,1,0:T(8,128)S(1)} %shard_map.73) | data formatting | bytes 262144

commit v5 on v4

--- a/solution.py
+++ b/solution.py
@@ -29,7 +29,6 @@
     prod,
     snd_c,
     rcv_c,
-    acc,
     snd_a1,
     rcv_a1,
     snd_b1,
@@ -176,9 +175,8 @@
         for t in range(slots):
             last = last + jnp.where(targets[t] <= s, 1, 0)
             below = below + jnp.where(targets[t] < s, 1, 0)
-        upto[s] = last
+        upto[s] = jnp.maximum(last - 1, 0)
         has[s] = jnp.where(last > below, 1.0, 0.0)
-    prod[0] = jnp.zeros(prod.shape[1:], F32)
 
     for cp in own_loads:
         cp.wait()
@@ -246,7 +244,10 @@
                 (((1,), (1,)), ((), ())),
                 preferred_element_type=F32,
             )
-            prod[n + 1] = total.reshape(prod.shape[1:]) + prod[n] * joins[n]
+            total = total.reshape(prod.shape[3:])
+            if n > 0:
+                total = total + prod[zh, w, n - 1] * joins[n]
+            prod[zh, w, n] = total
 
     def core_send(zh, w):
         return remote(
@@ -257,10 +258,8 @@
         @pl.loop(0, S * K)
         def _(s):
             y, k = s // K, s % K
-            away = prod[upto[s], co] * has[s]
-            kept = prod[upto[s], cm] * has[s]
+            away = prod[zh, w, upto[s], co] * has[s]
             snd_c[zh, w, y, k] = away.astype(BF16).reshape(X, Z2, B, H)
-            acc[zh, w, y, k] = kept.reshape(X, Z2, B, H)
 
         begin(core_send(zh, w))
 
@@ -302,7 +301,10 @@
         return remote(shares(held, rows), shares(held, rows), ssem, rsem, peer)
 
     def base(zh, w, y, k, x):
-        return acc[zh, w, y, k, x] + rcv_c[zh, w, y, k, x].astype(F32)
+        s = y * K + k
+        rows = pl.ds(pl.multiple_of(x * Z2 * B, Z2 * B), Z2 * B)
+        own = prod[zh, w, upto[s], cm, rows, :] * has[s]
+        return own.reshape(Z2, B, H) + rcv_c[zh, w, y, k, x].astype(F32)
 
     def a1_copy(zh, y):
         at = (zh, y)
@@ -324,9 +326,9 @@
         z = zh * Z2 + i
         slot = lax.rem(zm - z - 1 + 2 * Z, Z)
         return remote(
-            snd_z.at[zh, w, k, i],
+            snd_z.at[zh, i, w, k],
             rcv_z.at[w, k, slot],
-            z_send.at[zh, w, k, i],
+            z_send.at[zh, i],
             rz.at[w, k],
             dev(z, xm, cm, ym),
         )
@@ -367,7 +369,10 @@
             begin(b2_copy(zh, k))
 
     def z_own(zh, w, k, i):
-        total = acc[zh, w, ym, k, xm, i] + rcv_c[zh, w, ym, k, xm, i].astype(F32)
+        s = ym * K + k
+        rows = pl.ds(pl.multiple_of((xm * Z2 + i) * B, B), B)
+        total = prod[zh, w, upto[s], cm, rows, :] * has[s]
+        total = total + rcv_c[zh, w, ym, k, xm, i].astype(F32)
         if w == 0:
             total = total + rcv_a1[zh, ym, k, i].astype(F32)
             for d in range(1, S):
@@ -392,7 +397,7 @@
                 for i in range(Z2):
                     @pl.when(zm != zh * Z2 + i)
                     def _():
-                        snd_z[zh, w, k, i] = z_own(zh, w, k, i).astype(BF16)
+                        snd_z[zh, i, w, k] = z_own(zh, w, k, i).astype(BF16)
                         begin(z_copy(zh, w, k, i))
 
     def first_all(n_held, zh):
@@ -451,9 +456,8 @@
         for i in range(Z2):
             @pl.when(zm != zh * Z2 + i)
             def _():
-                for w in range(2):
-                    for k in range(K):
-                        z_copy(zh, w, k, i).wait_send()
+                ref = snd_z.at[zh, i]
+                remote(ref, ref, z_send.at[zh, i], f_recv.at[0], core_peer).wait_send()
 
 
 def local(mesh_sizes, wave, left, right, source, target, live, sector_rows):
@@ -476,10 +480,9 @@
         vm((slots, 2, 2, X, Z2, B, R), BF16),
         vm((slots, C, C), BF16),
         vm((slots, 2, R // 2, C), BF16),
-        vm((slots + 1, 2, X * Z2 * B, H), F32),
+        vm((2, 2, slots, 2, X * Z2 * B, H), F32),
         vm((2, 2, S, K, X, Z2, B, H), BF16),
         vm((2, 2, S, K, X, Z2, B, H), BF16),
-        vm((2, 2, S, K, X, Z2, B, H), F32),
         vm((2, S) + share, BF16),
         vm((2, S) + share, BF16),
         vm((2, 2, S - 1) + share, BF16),
@@ -488,7 +491,7 @@
         vm((2, S - 1) + share, BF16),
         vm((2,) + share, BF16),
         vm((2,) + share, BF16),
-        vm((2, 2) + share, BF16),
+        vm((2, Z2, 2, K, B, H), BF16),
         vm((2, K, Z - 1, B, H), BF16),
         pltpu.SMEM((slots,), jnp.int32),
         pltpu.SMEM((slots,), F32),
@@ -502,7 +505,7 @@
         dma((S - 1, K, RELAYED)),
         dma((2,)),
         dma((5,)),
-        dma((2, 2, K, Z2)),
+        dma((2, Z2)),
         dma((2, 2)),
         dma((2, S)),
         dma((2, 2, S - 1)),

time: 35.4 us -> 35.2 us (level)
  no operation moved by 1% of the time
where the time goes in v5:
time: 35.2 us; the launch traced here: 35.1 us
  Pallas kernels  33 us (94%)
  other arithmetic  0.77 us (2%)
  local copies, waits for them, and re-layouts  0.66 us (2%)
  between operations  0.66 us (2%)
    pallas_call x1, Pallas kernels, local(): pl.pallas_call(functools.partial(kernel, dims), out_shape=jax.ShapeDtypeS...  33 us
    concatenate x1, other arithmetic, local(): jnp.concatenate([source, target, live, sector_rows])  0.77 us

profile of v5, /device:TPU:24, one launch (start us, length us, event | category | flops | bytes accessed | tf_op | source)
XLA Modules:
  0.0 35.1 jit_solution(4230493914366438777)
XLA Ops:
  0.7 0.8 %pad_add_fusion.packed = s32[21]{0:T(128)S(1)} fusion(s32[4]{0:T(128)} %param.13, s32[1]{0:T(128)S(6)} %copy.9, s32[8]{0:T(128)} %param.11, s32[8]{0:T(128)} %param.10), kind=kLoop, calls=%fused_computation | loop fusion | flops 63 | bytes 168 | tf_op jit(solution)/shard_map/concatenate | solution.py:527
  1.4 33.0 %shard_map.73 = f32[2,32,512]{2,1,0:T(8,128)S(1)} custom-call(bf16[2,512,512]{2,1,0:T(8,128)(2,1)} %wave.1, bf16[8,2,2,2,2,32,512]{6,5,4,3,2,1,0:T(8,128)(2,1)} %bitcast.1, bf16[8,512,512]{2,1,0:T(8,128)(2,1)} %right.1, s32[21]{0:T(128)S(1)} %pad_add_fusion.packed), custom_call_target="tpu_custom_call" | custom-call | tf_op jit(solution)/shard_map/pallas_call | solution.py:518
  34.4 0.7 %copy.10 = f32[2,32,512]{2,1,0:T(8,128)} copy(f32[2,32,512]{2,1,0:T(8,128)S(1)} %shard_map.73) | data formatting | bytes 262144

commit v6 on v5

--- a/solution.py
+++ b/solution.py
@@ -11,7 +11,7 @@
 F32 = jnp.float32
 STEPS = 8
 RELAYED = 5
-LAG = 8
+LAG = 4
 
 
 def kernel(
@@ -186,41 +186,41 @@
 
     step = R // STEPS
     tail = (STEPS - RELAYED) * step
-    pieces = [(d, k, j) for k in range(K) for j in range(RELAYED) for d in range(1, S)]
-    tails = [(d, k) for k in range(K) for d in range(1, S)]
+    pieces = [(d, j) for j in range(RELAYED) for d in range(1, S)]
+    tails = list(range(1, S))
 
     def begin(*copies):
         for cp in copies:
             cp.start()
 
-    def part(held, d, k, j, c):
-        sector = lax.rem(ym + S - d, S) * K + k
+    def part(held, d, j, c):
+        sectors = pl.ds(lax.rem(ym + S - d, S) * K, K)
         rows = pl.ds(RELAYED * step, tail) if j == RELAYED else pl.ds(j * step, step)
-        return held.at[sector, rows, pl.ds(pl.multiple_of(c * Q, 128), Q)]
-
-    def y_copy(d, k, j, source):
-        ref = part(near, source, k, j, cm)
-        return remote(ref, ref, g_send.at[0], g_recv.at[d - 1, k, j], y_peer(d))
-
-    def y_far(d, k, source):
-        ref = part(far, source, k, RELAYED, cm)
-        return remote(ref, ref, g_send.at[1], e_recv.at[d - 1, k], y_peer(d))
-
-    def x_copy(d, k, j):
-        ref = part(near, d, k, j, cm)
-        dst = part(far, d, k, j, cm)
-        return remote(ref, dst, g_send.at[2], h_recv.at[d - 1, k, j], x_peer)
-
-    def core_copy(d, k, j, n, c):
-        ref = part((near, far)[n], d, k, j, c)
+        return held.at[sectors, rows, pl.ds(pl.multiple_of(c * Q, 128), Q)]
+
+    def y_copy(d, j, source):
+        ref = part(near, source, j, cm)
+        return remote(ref, ref, g_send.at[0], g_recv.at[d - 1, j], y_peer(d))
+
+    def y_far(d, source):
+        ref = part(far, source, RELAYED, cm)
+        return remote(ref, ref, g_send.at[1], e_recv.at[d - 1], y_peer(d))
+
+    def x_copy(d, j):
+        ref = part(near, d, j, cm)
+        dst = part(far, d, j, cm)
+        return remote(ref, dst, g_send.at[2], h_recv.at[d - 1, j], x_peer)
+
+    def core_copy(d, j, n, c):
+        ref = part((near, far)[n], d, j, c)
         return remote(ref, ref, g_send.at[3 + n], f_recv.at[n], core_peer)
 
-    for d, k, j in pieces:
-        begin(y_copy(d, k, j, 0))
-    for d, k in tails:
-        begin(y_copy(d, k, RELAYED, 0))
-    for d, k in tails:
-        begin(y_far(d, k, 0))
+    for d, j in pieces:
+        begin(y_copy(d, j, 0))
+    for d in tails:
+        begin(y_copy(d, RELAYED, 0))
+    for d in tails:
+        begin(y_far(d, 0))
 
     depth_ids = lax.broadcasted_iota(jnp.int32, (1, R), 1)
     chunk = 4 if slots % 4 == 0 else slots
@@ -266,28 +266,28 @@
     handled = []
 
     def relay_far(count):
-        for d, k, j in pieces[len(handled) : len(handled) + count]:
-            x_copy(d, k, j).wait_recv()
-            begin(core_copy(d, k, j, 1, cm))
-            handled.append((d, k, j))
-
-    for n, (d, k, j) in enumerate(pieces):
-        y_copy(d, k, j, d).wait_recv()
-        begin(x_copy(d, k, j), core_copy(d, k, j, 0, cm))
+        for d, j in pieces[len(handled) : len(handled) + count]:
+            x_copy(d, j).wait_recv()
+            begin(core_copy(d, j, 1, cm))
+            handled.append((d, j))
+
+    for n, (d, j) in enumerate(pieces):
+        y_copy(d, j, d).wait_recv()
+        begin(x_copy(d, j), core_copy(d, j, 0, cm))
         if n >= LAG:
             relay_far(1)
-    for d, k in tails:
-        y_copy(d, k, RELAYED, d).wait_recv()
-        begin(core_copy(d, k, RELAYED, 0, cm))
+    for d in tails:
+        y_copy(d, RELAYED, d).wait_recv()
+        begin(core_copy(d, RELAYED, 0, cm))
         relay_far(1)
     if Z > 2:
         pl.semaphore_wait(ready.at[0], z_sides)
         if Z > 3:
             signal_sides(ready.at[1])
     relay_far(len(pieces))
-    for d, k in tails:
-        y_far(d, k, d).wait_recv()
-        begin(core_copy(d, k, RELAYED, 1, cm))
+    for d in tails:
+        y_far(d, d).wait_recv()
+        begin(core_copy(d, RELAYED, 1, cm))
     pltpu.make_async_copy(lbuf, lbuf, load_sem.at[3]).wait()
     pltpu.make_async_copy(rbuf, rbuf, load_sem.at[4]).wait()
     others = pl.ds(0, (S - 1) * K)
@@ -500,9 +500,9 @@
         dma((5,)),
         pltpu.SemaphoreType.REGULAR((max(Z - 2, 1),)),
         dma((5,)),
-        dma((S - 1, K, RELAYED + 1)),
-        dma((S - 1, K)),
-        dma((S - 1, K, RELAYED)),
+        dma((S - 1, RELAYED + 1)),
+        dma((S - 1,)),
+        dma((S - 1, RELAYED)),
         dma((2,)),
         dma((5,)),
         dma((2, Z2)),

time: 35.2 us -> 35.1 us (level)
  no operation moved by 1% of the time
where the time goes in v6:
time: 35.1 us; the launch traced here: 34.9 us
  Pallas kernels  32.9 us (94%)
  other arithmetic  0.77 us (2%)
  local copies, waits for them, and re-layouts  0.66 us (2%)
  between operations  0.66 us (2%)
    pallas_call x1, Pallas kernels, local(): pl.pallas_call(functools.partial(kernel, dims), out_shape=jax.ShapeDtypeS...  32.9 us
    concatenate x1, other arithmetic, local(): jnp.concatenate([source, target, live, sector_rows])  0.77 us

profile of v6, /device:TPU:24, one launch (start us, length us, event | category | flops | bytes accessed | tf_op | source)
XLA Modules:
  0.0 34.9 jit_solution(7713055519124179579)
XLA Ops:
  0.7 0.8 %pad_add_fusion.packed = s32[21]{0:T(128)S(1)} fusion(s32[4]{0:T(128)} %param.13, s32[1]{0:T(128)S(6)} %copy.9, s32[8]{0:T(128)} %param.11, s32[8]{0:T(128)} %param.10), kind=kLoop, calls=%fused_computation | loop fusion | flops 63 | bytes 168 | tf_op jit(solution)/shard_map/concatenate | solution.py:527
  1.4 32.9 %shard_map.73 = f32[2,32,512]{2,1,0:T(8,128)S(1)} custom-call(bf16[2,512,512]{2,1,0:T(8,128)(2,1)} %wave.1, bf16[8,2,2,2,2,32,512]{6,5,4,3,2,1,0:T(8,128)(2,1)} %bitcast.1, bf16[8,512,512]{2,1,0:T(8,128)(2,1)} %right.1, s32[21]{0:T(128)S(1)} %pad_add_fusion.packed), custom_call_target="tpu_custom_call" | custom-call | tf_op jit(solution)/shard_map/pallas_call | solution.py:518
  34.3 0.7 %copy.10 = f32[2,32,512]{2,1,0:T(8,128)} copy(f32[2,32,512]{2,1,0:T(8,128)S(1)} %shard_map.73) | data formatting | bytes 262144

commit v7 on v6

--- a/solution.py
+++ b/solution.py
@@ -9,9 +9,9 @@
 
 BF16 = jnp.bfloat16
 F32 = jnp.float32
-STEPS = 8
-RELAYED = 5
-LAG = 4
+STEPS = 16
+RELAYED = 11
+LAG = 9
 
 
 def kernel(
@@ -255,7 +255,7 @@
         )
 
     def spread(zh, w):
-        @pl.loop(0, S * K)
+        @pl.loop(0, S * K, unroll=4)
         def _(s):
             y, k = s // K, s % K
             away = prod[zh, w, upto[s], co] * has[s]

time: 35.1 us -> 35 us (level)
  Pallas kernels: 32.9 us -> 32.5 us
where the time goes in v7:
time: 35 us; the launch traced here: 34.6 us
  Pallas kernels  32.5 us (93%)
  other arithmetic  0.77 us (2%)
  local copies, waits for them, and re-layouts  0.66 us (2%)
  between operations  0.66 us (2%)
    pallas_call x1, Pallas kernels, local(): pl.pallas_call(functools.partial(kernel, dims), out_shape=jax.ShapeDtypeS...  32.5 us
    concatenate x1, other arithmetic, local(): jnp.concatenate([source, target, live, sector_rows])  0.77 us

profile of v7, /device:TPU:24, one launch (start us, length us, event | category | flops | bytes accessed | tf_op | source)
XLA Modules:
  0.0 34.6 jit_solution(11249744372262629143)
XLA Ops:
  0.7 0.8 %pad_add_fusion.packed = s32[21]{0:T(128)S(1)} fusion(s32[4]{0:T(128)} %param.13, s32[1]{0:T(128)S(6)} %copy.9, s32[8]{0:T(128)} %param.11, s32[8]{0:T(128)} %param.10), kind=kLoop, calls=%fused_computation | loop fusion | flops 63 | bytes 168 | tf_op jit(solution)/shard_map/concatenate | solution.py:527
  1.4 32.5 %shard_map.73 = f32[2,32,512]{2,1,0:T(8,128)S(1)} custom-call(bf16[2,512,512]{2,1,0:T(8,128)(2,1)} %wave.1, bf16[8,2,2,2,2,32,512]{6,5,4,3,2,1,0:T(8,128)(2,1)} %bitcast.1, bf16[8,512,512]{2,1,0:T(8,128)(2,1)} %right.1, s32[21]{0:T(128)S(1)} %pad_add_fusion.packed), custom_call_target="tpu_custom_call" | custom-call | tf_op jit(solution)/shard_map/pallas_call | solution.py:518
  34.0 0.7 %copy.10 = f32[2,32,512]{2,1,0:T(8,128)} copy(f32[2,32,512]{2,1,0:T(8,128)S(1)} %shard_map.73) | data formatting | bytes 262144

commit v8 on v7

--- a/solution.py
+++ b/solution.py
@@ -11,7 +11,7 @@
 F32 = jnp.float32
 STEPS = 16
 RELAYED = 11
-LAG = 9
+LAG = 11
 
 
 def kernel(

time: 35 us -> 35 us (level)
  no operation moved by 1% of the time
where the time goes in v8:
time: 35 us; the launch traced here: 34.6 us
  Pallas kernels  32.5 us (93%)
  other arithmetic  0.77 us (2%)
  local copies, waits for them, and re-layouts  0.66 us (2%)
  between operations  0.66 us (2%)
    pallas_call x1, Pallas kernels, local(): pl.pallas_call(functools.partial(kernel, dims), out_shape=jax.ShapeDtypeS...  32.5 us
    concatenate x1, other arithmetic, local(): jnp.concatenate([source, target, live, sector_rows])  0.77 us

profile of v8, /device:TPU:24, one launch (start us, length us, event | category | flops | bytes accessed | tf_op | source)
XLA Modules:
  0.0 34.6 jit_solution(6047400546655764038)
XLA Ops:
  0.7 0.8 %pad_add_fusion.packed = s32[21]{0:T(128)S(1)} fusion(s32[4]{0:T(128)} %param.13, s32[1]{0:T(128)S(6)} %copy.9, s32[8]{0:T(128)} %param.11, s32[8]{0:T(128)} %param.10), kind=kLoop, calls=%fused_computation | loop fusion | flops 63 | bytes 168 | tf_op jit(solution)/shard_map/concatenate | solution.py:527
  1.4 32.5 %shard_map.73 = f32[2,32,512]{2,1,0:T(8,128)S(1)} custom-call(bf16[2,512,512]{2,1,0:T(8,128)(2,1)} %wave.1, bf16[8,2,2,2,2,32,512]{6,5,4,3,2,1,0:T(8,128)(2,1)} %bitcast.1, bf16[8,512,512]{2,1,0:T(8,128)(2,1)} %right.1, s32[21]{0:T(128)S(1)} %pad_add_fusion.packed), custom_call_target="tpu_custom_call" | custom-call | tf_op jit(solution)/shard_map/pallas_call | solution.py:518
  34.0 0.7 %copy.10 = f32[2,32,512]{2,1,0:T(8,128)} copy(f32[2,32,512]{2,1,0:T(8,128)S(1)} %shard_map.73) | data formatting | bytes 262144
